TPU v7x, 32 devices: a whole 2x2x4 slice. The times are simulated.
32 devices in a mesh: facet: 8 (over z, y), freq: 4 (over x, core).
Axes of the slice: x: 2, y: 2, z: 4, core: 2. Of those that a mesh axis runs over, the one named last changes fastest.
Arguments:
- visibilities: bfloat16 [4, 2048, 2, 512], P('freq', 'facet'), may hold values from -6 to 6
- uvw: bfloat16 [4, 2048, 3, 512], P('freq', 'facet'), may hold values from -4 to 4
- facet_of: int32 [4, 2048, 1], P('freq', 'facet'), may hold values from 0 to 7; in each aligned block of 256 rows (0 to 255, 256 to 511, ..., all dimensions but the last counted through in order) at most 128 rows name the same one
- plane_of: int32 [4, 2048], P('freq', 'facet'), may hold values from 0 to 7
- cell_of: int32 [4, 2048], P('freq', 'facet'), may hold values from 0 to 1023
- kernels: bfloat16 [8, 2, 512, 256], replicated, may hold values from -0.25 to 0.25
- centers: float32 [8, 2], replicated, may hold values from -0.4 to 0.4
Outputs:
- images: float32 [8, 512, 512], P('facet', None, 'freq')
Inputs may be any that keep to these rules, and one draw needn't show every extreme that they name: `facet_of`: the facet index k is held by index k of the facet axis. In each aligned block of 256 tiles of one group, no facet is named by more than 128 tiles, and in some blocks one facet is named by exactly 128.
All inputs are finite; a program needn't handle non-finite values.
Results may differ from a plain program's by a relative error of at most 0.0095.
Values may be sent and summed in bfloat16 or wider, within the bound.
No kernel may reach another device: no remote copies, remote signals or barrier semaphores. Data moves between devices by JAX's collectives and lax.ppermute only.
A program may use at most 128 MiB of HBM per device.

v0:
```python
import functools

import jax
import jax.numpy as jnp
import numpy as np
from jax import lax
from jax.experimental import pallas as pl
from jax.experimental.pallas import tpu as pltpu
from jax.sharding import PartitionSpec as P


GRID = 512
PSIDE = 16
NBLK = GRID // PSIDE
LANES = 128
SUBLANES = 8

SIN_POLY = (4.442882919124345, -7.30824568650904, 3.6063542184326933, -0.8461116503732697, 0.10982451642490525)
COS_POLY = (1.4142134962552284, -6.978850948563788, 5.73946037690675, -1.8835579059841707, 0.3106880275217573)


def horner(square, coefficients):
    value = coefficients[-1] * square + coefficients[-2]
    for coefficient in coefficients[-3::-1]:
        value = value * square + coefficient
    return value


def cos_sin_turns(turns):
    rest = turns - jnp.round(turns)
    square = rest * rest
    sine = rest * horner(square, SIN_POLY)
    return (1.0 - sine * sine, sine * horner(square, COS_POLY))


def compiler_params(mebibytes):
    return pltpu.CompilerParams(vmem_limit_bytes=mebibytes << 20)


VMEM = pl.BlockSpec(memory_space=pltpu.VMEM)
HBM = pl.BlockSpec(memory_space=pltpu.HBM)


def dft_tables(length):
    indices = jnp.arange(length, dtype=jnp.int32)
    products_mod = indices[:, None] * indices[None, :] % length
    angle_table = products_mod.astype(jnp.float32) * (2.0 * jnp.pi / length)
    norm_scale = 1.0 / jnp.sqrt(jnp.float32(length))
    table_real = (jnp.cos(angle_table) * norm_scale).astype(jnp.bfloat16)
    table_imag = (jnp.sin(angle_table) * norm_scale).astype(jnp.bfloat16)
    return (table_real, table_imag)


def rotate_tiles(vis_pair, coords, sky_pos):
    l_coord = sky_pos[:, 0:1]
    m_coord = sky_pos[:, 1:2]
    w_term = jnp.sqrt(1.0 - l_coord * l_coord - m_coord * m_coord) - 1.0
    coords = coords.astype(jnp.float32)
    phase_angle = (
        2.0 * jnp.pi * (l_coord * coords[:, 0] + m_coord * coords[:, 1] + w_term * coords[:, 2])
    )
    cosine = jnp.cos(phase_angle)
    sine_part = jnp.sin(phase_angle)
    real_part = vis_pair[:, 0].astype(jnp.float32)
    imag_part = vis_pair[:, 1].astype(jnp.float32)
    rot_real = (real_part * cosine + imag_part * sine_part).astype(jnp.bfloat16)
    rot_imag = (imag_part * cosine - real_part * sine_part).astype(jnp.bfloat16)
    return (rot_real, rot_imag)


def stack_kernels(kernels):
    kern_real = kernels[:, 0]
    kern_imag = kernels[:, 1]
    upper_rows = jnp.concatenate([kern_real, kern_imag], axis=2)
    lower_rows = jnp.concatenate([-kern_imag, kern_real], axis=2)
    stacked_rows = jnp.concatenate([upper_rows, lower_rows], axis=0)
    return stacked_rows.reshape(-1, stacked_rows.shape[2])


def grid_tiles(rot_real, rot_imag, planes, stacked, plane_count):
    plane_select = (planes[:, None] == jnp.arange(plane_count)[None, :]).astype(jnp.bfloat16)
    spread = jnp.concatenate(
        [
            rot_real[:, None, :] * plane_select[:, :, None],
            rot_imag[:, None, :] * plane_select[:, :, None],
        ],
        axis=1,
    )
    spread = spread.reshape(spread.shape[0], -1)
    return jnp.dot(spread, stacked, preferred_element_type=jnp.float32).astype(jnp.bfloat16)


def shards(visibilities, uvw, facet_of, plane_of, cell_of, kernels, centers):
    peer_count = lax.axis_size("facet")
    tile_count = visibilities.shape[1]
    capacity = 4 * tile_count // peer_count
    total_slots = peer_count * capacity
    vis_pair = visibilities[0]
    coords = uvw[0]
    target = facet_of[0, :, 0]
    planes = plane_of[0]
    tile_cells = cell_of[0]
    plane_count = kernels.shape[0]
    stacked = stack_kernels(kernels)
    dest_hits = (target[:, None] == jnp.arange(peer_count)[None, :]).astype(jnp.int32)
    before = jnp.cumsum(dest_hits, axis=0) - dest_hits
    within_rank = jnp.sum(before * dest_hits, axis=1)
    slot_index = target * capacity + within_rank
    chosen = (target[:, None] == jnp.arange(centers.shape[0])[None, :]).astype(jnp.float32)
    sky_rows = jnp.sum(chosen[:, :, None] * centers[None, :, :], axis=1)
    rot_real, rot_imag = rotate_tiles(vis_pair, coords, sky_rows)
    own_patches = grid_tiles(rot_real, rot_imag, planes, stacked, plane_count)
    patch_buffer = (
        jnp.zeros((total_slots, own_patches.shape[1]), jnp.bfloat16).at[slot_index].set(own_patches)
    )
    cell_buffer = jnp.zeros((total_slots,), jnp.int32).at[slot_index].set(tile_cells)
    patches, slot_cells = (
        lax.all_to_all(
            patch_buffer.reshape(peer_count, capacity, -1),
            "facet",
            split_axis=0,
            concat_axis=0,
            tiled=True,
        ),
        lax.all_to_all(
            cell_buffer.reshape(peer_count, capacity),
            "facet",
            split_axis=0,
            concat_axis=0,
            tiled=True,
        ),
    )
    patches = patches.reshape(-1, patches.shape[-1])
    slot_cells = slot_cells.reshape(-1)
    nblocks = GRID // PSIDE
    ncells = nblocks * nblocks
    placing = (slot_cells[None, :] == jnp.arange(ncells)[:, None]).astype(jnp.bfloat16)
    blocks = jnp.dot(placing, patches, preferred_element_type=jnp.float32).astype(jnp.bfloat16)
    uv_grid = (
        blocks.reshape(nblocks, nblocks, 2, PSIDE, PSIDE)
        .transpose(2, 0, 3, 1, 4)
        .reshape(2 * GRID, GRID)
    )
    table_real, table_imag = dft_tables(GRID)
    table_both = jnp.concatenate([table_real, table_imag], axis=1)
    product = jnp.dot(uv_grid, table_both, preferred_element_type=jnp.float32)
    half_real = product[:GRID, :GRID] - product[GRID:, GRID:]
    half_imag = product[:GRID, GRID:] + product[GRID:, :GRID]
    partial_value = jnp.stack([half_real, half_imag]).astype(jnp.bfloat16)
    summed = lax.psum_scatter(
        partial_value.astype(jnp.float32).astype(jnp.bfloat16),
        "freq",
        scatter_dimension=2,
        tiled=True,
    )
    right_side = jnp.concatenate([summed[0], -summed[1]], axis=0)
    facet_image = jnp.dot(table_both, right_side, preferred_element_type=jnp.float32)
    return facet_image[None]


def gather_kernel(peers, sizes, centers_hbm, facet_hbm, plane_hbm, cell_hbm, vis_hbm, uvw_hbm, kern_hbm, *rest):
    out_refs = rest[: len(sizes)]
    centers_ref, facet_ref, plane_ref, cell_ref, vis_ref, uvw_ref, kern_ref, parts_ref, rows_ref, sems = rest[len(sizes) :]
    planes, _, depth, cells = kern_ref.shape
    tiles = facet_ref.shape[1]
    half = tiles // 2
    groups_of_lanes = depth // LANES
    rows_of = [slice(h * half, (h + 1) * half) for h in range(2)]
    vis_rows = vis_ref.shape[0] // 2
    transfers = [(centers_hbm, centers_ref), (facet_hbm, facet_ref), (plane_hbm, plane_ref)]
    for h in range(2):
        part = slice(h * vis_rows, (h + 1) * vis_rows)
        transfers += [(vis_hbm.at[part], vis_ref.at[part]), (uvw_hbm.at[:, rows_of[h]], uvw_ref.at[:, rows_of[h]])]
    transfers += [(cell_hbm, cell_ref)] + [(kern_hbm.at[p], kern_ref.at[p]) for p in range(planes)]
    copies = [pltpu.make_async_copy(source, target, sems.at[i]) for i, (source, target) in enumerate(transfers)]
    for copy in copies:
        copy.start()
    for copy in copies[:3]:
        copy.wait()
    facet = facet_ref[...]
    l_row = jnp.zeros(facet.shape, jnp.float32)
    m_row = jnp.zeros(facet.shape, jnp.float32)
    for f in range(peers):
        hit = facet == f
        l_row = jnp.where(hit, centers_ref[0:1, f : f + 1], l_row)
        m_row = jnp.where(hit, centers_ref[1:2, f : f + 1], m_row)
    d_row = jnp.sqrt(1.0 - l_row * l_row - m_row * m_row) - 1.0
    plane_row = plane_ref[...].astype(jnp.float32)
    zero_row = jnp.zeros_like(l_row)
    columns = jnp.concatenate([l_row, m_row, d_row, plane_row] + [zero_row] * 4, axis=0).T

    near, capacity, few, slots = peers // 2, sizes[0], sizes[peers // 2], sum(sizes)
    relative = facet ^ lax.axis_index("facet")
    lanes = lax.broadcasted_iota(jnp.int32, (tiles, tiles), 1)
    earlier = (lax.broadcasted_iota(jnp.int32, (tiles, tiles), 0) < lanes).astype(jnp.float32).astype(jnp.bfloat16)
    facets = lax.broadcasted_iota(jnp.int32, (peers, tiles), 0)
    hits = facets == relative
    before = jnp.dot(hits.astype(jnp.float32).astype(jnp.bfloat16), earlier, preferred_element_type=jnp.float32)
    rank = jnp.sum(jnp.where(hits, before, 0.0), axis=0, keepdims=True).astype(jnp.int32)
    passed = jnp.where(facets >= near, jnp.maximum(before - few, 0.0), 0.0)
    passed = jnp.sum(passed, axis=0, keepdims=True).astype(jnp.int32)
    direct = near * capacity + (relative - near) * few + rank
    slot = jnp.where(rank < few, direct, near * (capacity + few) + passed)
    slot = jnp.where(relative < near, relative * capacity + rank, slot)

    patches = []
    for h in range(2):
        tile_rows = rows_of[h]
        for copy in copies[3:5] if h == 0 else copies[5:]:
            copy.wait()
        part = slice(h * vis_rows, (h + 1) * vis_rows)
        parts_ref[part] = vis_ref[part].astype(jnp.float32)
        l_col, m_col, d_col = (jnp.broadcast_to(columns[tile_rows, i : i + 1], (half, LANES)) for i in range(3))
        for j in range(groups_of_lanes):
            lane = slice(j * LANES, (j + 1) * LANES)
            u, v, w = (uvw_ref[i, tile_rows, lane].astype(jnp.float32) for i in range(3))
            cosine, sine = cos_sin_turns(l_col * u + m_col * v + d_col * w)
            first = 2 * (h * half * groups_of_lanes + j)
            real = parts_ref[pl.ds(first, half, stride=2 * groups_of_lanes), :]
            imag = parts_ref[pl.ds(first + 1, half, stride=2 * groups_of_lanes), :]
            rot_real = (real * cosine + imag * sine).astype(jnp.bfloat16)
            rot_imag = (imag * cosine - real * sine).astype(jnp.bfloat16)
            right = slice(depth + j * LANES, depth + (j + 1) * LANES)
            rows_ref[h, :half, lane] = rot_real
            rows_ref[h, :half, right] = -rot_imag
            rows_ref[h, half:, lane] = rot_imag
            rows_ref[h, half:, right] = rot_real
    for h in range(2):
        plane_two = jnp.concatenate([columns[rows_of[h], 3:4]] * 2, axis=0)
        total = None
        for p in range(planes):
            mask = (plane_two == float(p)).astype(jnp.float32).astype(jnp.bfloat16)
            product = jnp.dot(
                rows_ref[h] * mask, kern_ref[p].reshape(2 * depth, cells), preferred_element_type=jnp.float32
            )
            total = product if total is None else total + product
        patches.append(jnp.concatenate([total[:half], total[half:]], axis=1).astype(jnp.bfloat16))
    patches = jnp.concatenate(patches, axis=0)
    placing = lax.broadcasted_iota(jnp.int32, (slots, tiles), 0) == slot
    placing = placing.astype(jnp.float32).astype(jnp.bfloat16)
    placed = jnp.dot(placing, patches, preferred_element_type=jnp.float32).astype(jnp.bfloat16)
    cell = cell_ref[...].astype(jnp.float32)
    block_u = jnp.floor(cell * (1.0 / NBLK))
    block_v = cell - block_u * NBLK
    labels = [block_u, block_v, facet.astype(jnp.float32)] + [zero_row] * (SUBLANES - 3)
    labels = jnp.concatenate(labels, axis=0).astype(jnp.bfloat16)
    labels = lax.dot_general(labels, placing, (((1,), (1,)), ((), ())), preferred_element_type=jnp.float32)
    lane = lax.broadcasted_iota(jnp.int32, (SUBLANES, LANES), 1)
    start = 0
    for ref, size in zip(out_refs, sizes):
        for j in range(2 * cells // LANES):
            ref[j * size : (j + 1) * size, :] = placed[start : start + size, j * LANES : (j + 1) * LANES]
        tile = start // LANES * LANES
        inside = (lane >= start - tile) & (lane < start - tile + size)
        ref[2 * cells // LANES * size :, :] = jnp.where(inside, labels[:, tile : tile + LANES], 0.0).astype(jnp.bfloat16)
        start += size


def load_patches(in_refs, sizes, patch_buf):
    cells = PSIDE * PSIDE
    half_tiles = cells // LANES
    start = 0
    for ref, size in zip(in_refs, sizes):
        rows = slice(start, start + size)
        below = slice(sum(sizes) + start, sum(sizes) + start + size)
        for j in range(half_tiles):
            left = slice(j * LANES, (j + 1) * LANES)
            right = slice(cells + j * LANES, cells + (j + 1) * LANES)
            real = ref[j * size : (j + 1) * size, :]
            imag = ref[(half_tiles + j) * size : (half_tiles + j + 1) * size, :]
            patch_buf[rows, left] = real
            patch_buf[rows, right] = imag
            patch_buf[below, left] = -imag
            patch_buf[below, right] = real
        start += size


def cell_phases(in_refs, sizes, direct):
    labels, start = [], 0
    for ref, size in zip(in_refs, sizes):
        here = ref[2 * PSIDE * PSIDE // LANES * size :, :].astype(jnp.float32)
        if start % LANES:
            labels[-1] = labels[-1] + here
        else:
            labels.append(here)
        start += size
    labels = jnp.concatenate(labels, axis=1)
    lane = lax.broadcasted_iota(jnp.int32, (1, start), 1)
    mine = labels[2:3] == lax.axis_index("facet").astype(jnp.float32)
    mine = jnp.where(mine | (lane < sum(sizes[:direct])), 1.0, 0.0)
    index = lax.broadcasted_iota(jnp.int32, (NBLK, start), 0).astype(jnp.float32) * (1.0 / NBLK)
    cos_u, sin_u = cos_sin_turns(index * labels[0:1])
    return (cos_u * mine, sin_u * mine) + cos_sin_turns(index * labels[1:2])


def fill_phases(buf, rows_of, phases):
    cos_u, sin_u, cos_v, sin_v = phases
    slots = cos_v.shape[1]
    for i, j in enumerate(rows_of):
        cu, su = cos_u[j : j + 1], sin_u[j : j + 1]
        rows = slice(i * NBLK, (i + 1) * NBLK)
        buf[rows, :slots] = (cu * cos_v - su * sin_v).astype(jnp.bfloat16)
        buf[rows, slots:] = (cu * sin_v + su * cos_v).astype(jnp.bfloat16)


PER_CHUNK = 8


def spectrum_kernel(sizes, direct, *rest):
    count = len(sizes)
    in_refs, out_ref, (phases_buf, patch_buf) = rest[:count], rest[count], rest[count + 1 :]
    load_patches(in_refs, sizes, patch_buf)
    phases = cell_phases(in_refs, sizes, direct)
    width = PER_CHUNK * NBLK
    for chunk in range(NBLK // PER_CHUNK):
        buf = phases_buf.at[chunk % 2]
        fill_phases(buf, range(chunk * PER_CHUNK, (chunk + 1) * PER_CHUNK), phases)
        out_ref[chunk * width : (chunk + 1) * width, :] = jnp.dot(
            buf[...], patch_buf[...], preferred_element_type=jnp.float32
        )


def image_kernel(sizes, direct, groups, table_ref, early_ref, *rest):
    count = len(sizes)
    in_refs, out_refs = rest[:count], rest[count : count + groups]
    phases_buf, patch_buf, table_buf = rest[count + groups :]
    cells = PSIDE * PSIDE
    share = cells // groups
    load_patches(in_refs, sizes, patch_buf)
    for s in range(groups):
        start = pl.multiple_of((lax.axis_index("freq") ^ s) * share, share)
        table_buf[s * share : (s + 1) * share, :] = table_ref[pl.ds(start, share), :]
    phases = cell_phases(in_refs, sizes, direct)

    lane = lax.broadcasted_iota(jnp.int32, (NBLK, cells), 1)
    row = lax.broadcasted_iota(jnp.int32, (NBLK, cells), 0)
    patch_u, patch_v = lane // PSIDE, lane % PSIDE
    twid_u = cos_sin_turns((row * patch_u).astype(jnp.float32) * (1.0 / GRID))
    twid_v = cos_sin_turns((row * patch_v).astype(jnp.float32) * (1.0 / GRID))

    width = PER_CHUNK * NBLK
    for chunk in range(NBLK // PER_CHUNK):
        buf = phases_buf.at[chunk % 2]
        fill_phases(buf, range(chunk * PER_CHUNK, (chunk + 1) * PER_CHUNK), phases)
        here = slice(chunk * width, (chunk + 1) * width)
        spectrum = early_ref[here, :] + jnp.dot(buf[...], patch_buf[...], preferred_element_type=jnp.float32)
        turned = []
        for i in range(PER_CHUNK):
            j = chunk * PER_CHUNK + i
            rows = slice(i * NBLK, (i + 1) * NBLK)
            real, imag = spectrum[rows, :cells], spectrum[rows, cells:]
            tr = twid_u[0][j : j + 1] * twid_v[0] - twid_u[1][j : j + 1] * twid_v[1]
            ti = twid_u[0][j : j + 1] * twid_v[1] + twid_u[1][j : j + 1] * twid_v[0]
            turned.append(jnp.concatenate([real * tr - imag * ti, real * ti + imag * tr], axis=1).astype(jnp.bfloat16))
        turned = jnp.concatenate(turned, axis=0)
        image = lax.dot_general(
            table_buf[...], turned, (((1,), (1,)), ((), ())), preferred_element_type=jnp.float32
        ).astype(jnp.bfloat16)
        for s in range(groups):
            out_refs[s][:, here] = image[s * share : (s + 1) * share]


def finish_kernel(groups, *refs):
    in_refs, out_ref = refs[:groups], refs[groups]
    columns = PSIDE // groups
    per_tile = LANES // NBLK
    lane = lax.broadcasted_iota(jnp.int32, (PSIDE, LANES), 1) // NBLK
    for tile in range(NBLK // per_tile):
        lanes = slice(tile * LANES, (tile + 1) * LANES)
        total = in_refs[0][:, lanes].astype(jnp.float32)
        for ref in in_refs[1:]:
            total = total + ref[:, lanes].astype(jnp.float32)
        for i in range(per_tile):
            value = jnp.zeros((PSIDE, LANES), jnp.float32)
            for kq in range(columns):
                piece = total[kq * PSIDE : (kq + 1) * PSIDE]
                shift = (kq - i) * NBLK % LANES
                piece = pltpu.roll(piece, shift, 1) if shift else piece
                value = jnp.where(lane == kq, piece, value)
            out_ref[pl.ds(tile * per_tile + i, PSIDE, stride=NBLK), :] = value


def patch_table():
    index = np.arange(PSIDE)
    kq, jq = (a.reshape(-1, 1) for a in np.meshgrid(index, index, indexing="ij"))
    pu, pv = (a.reshape(1, -1) for a in np.meshgrid(index, index, indexing="ij"))
    angle = 2.0 * np.pi * ((pu * jq + pv * kq) % PSIDE) / PSIDE
    return np.concatenate([np.cos(angle), -np.sin(angle)], axis=1) / GRID


def swap(piece, axis, distance):
    count = lax.axis_size(axis)
    return lax.ppermute(piece, axis, [(i, i ^ distance) for i in range(count)])


def packed_shards(visibilities, uvw, facet_of, plane_of, cell_of, kernels, centers):
    peers, groups = lax.axis_size("facet"), lax.axis_size("freq")
    tiles = visibilities.shape[1]
    capacity = 4 * tiles // peers
    planes, _, depth, cells = kernels.shape
    near = peers // 2
    sizes = [capacity] * near + [capacity // 2] * near + [tiles // 2]
    payloads = [jax.ShapeDtypeStruct((2 * cells // LANES * size + SUBLANES, LANES), jnp.bfloat16) for size in sizes]
    lanes = depth // LANES
    vis_rows = visibilities[0].reshape(tiles, 2, lanes, LANES).transpose(0, 2, 1, 3).reshape(-1, LANES)
    operands = (
        centers.T,
        facet_of.reshape(1, tiles),
        plane_of,
        cell_of,
        vis_rows,
        uvw[0].transpose(1, 0, 2),
        kernels,
    )
    pieces = pl.pallas_call(
        functools.partial(gather_kernel, peers, sizes),
        out_shape=payloads,
        in_specs=[HBM] * len(operands),
        out_specs=[VMEM] * len(sizes),
        scratch_shapes=[pltpu.VMEM(operand.shape, operand.dtype) for operand in operands]
        + [
            pltpu.VMEM(vis_rows.shape, jnp.float32),
            pltpu.VMEM((2, tiles, 2 * depth), jnp.bfloat16),
            pltpu.SemaphoreType.DMA((len(operands) + 1 + planes,)),
        ],
        compiler_params=compiler_params(40),
        name="gather",
    )(*(pltpu.with_memory_space_constraint(operand, pltpu.HBM) for operand in operands))
    overflow = [swap(pieces[peers], "facet", near)]
    received = [pieces[0]] + [swap(pieces[s], "facet", s) for s in range(1, peers)]
    overflow += [swap(overflow[0], "facet", s) for s in range(1, near)]
    early, late = received[:near] + overflow[:1], received[near:] + overflow[1:]
    early_sizes, late_sizes = sizes[:near] + sizes[peers:], sizes[near:peers] + sizes[peers:] * (near - 1)
    share = cells // groups
    points = NBLK * NBLK

    def buffers_and_cost(slots):
        buffers = [
            pltpu.VMEM((2, PER_CHUNK * NBLK, 2 * slots), jnp.bfloat16),
            pltpu.VMEM((2 * slots, 2 * cells), jnp.bfloat16),
        ]
        return buffers, pl.CostEstimate(flops=8 * points * slots * cells, bytes_accessed=4 << 20, transcendentals=0)

    buffers, cost = buffers_and_cost(sum(early_sizes))
    spectrum = pl.pallas_call(
        functools.partial(spectrum_kernel, early_sizes, near),
        out_shape=jax.ShapeDtypeStruct((points, 2 * cells), jnp.float32),
        in_specs=[VMEM] * len(early),
        out_specs=VMEM,
        scratch_shapes=buffers,
        compiler_params=compiler_params(40),
        cost_estimate=cost,
        name="spectrum",
    )(*early)
    buffers, cost = buffers_and_cost(sum(late_sizes))
    image = jax.ShapeDtypeStruct((share, points), jnp.bfloat16)
    images = pl.pallas_call(
        functools.partial(image_kernel, late_sizes, near, groups),
        out_shape=[image] * groups,
        in_specs=[VMEM] * (2 + len(late)),
        out_specs=[VMEM] * groups,
        scratch_shapes=buffers + [pltpu.VMEM((cells, 2 * cells), jnp.bfloat16)],
        compiler_params=compiler_params(40),
        cost_estimate=cost,
        name="image",
    )(jnp.asarray(patch_table(), jnp.bfloat16), spectrum, *late)
    summed = [images[0]] + [swap(images[s], "freq", s) for s in range(1, groups)]
    facet_image = pl.pallas_call(
        functools.partial(finish_kernel, groups),
        out_shape=jax.ShapeDtypeStruct((GRID, GRID // groups), jnp.float32),
        in_specs=[VMEM] * groups,
        out_specs=VMEM,
        compiler_params=compiler_params(16),
        name="finish",
    )(*summed)
    return facet_image[None]


def solution(mesh):
    in_specs = (
        P("freq", "facet", None, None),
        P("freq", "facet", None, None),
        P("freq", "facet", None),
        P("freq", "facet"),
        P("freq", "facet"),
        P(),
        P(),
    )
    out_specs = P("facet", None, "freq")

    def body(*args):
        peers, groups = lax.axis_size("facet"), lax.axis_size("freq")
        capacity = 4 * args[0].shape[1] // peers
        powers = peers & (peers - 1) == 0 and groups & (groups - 1) == 0
        packed = capacity == LANES and powers and GRID // groups == LANES
        return (packed_shards if packed else shards)(*args)

    return jax.shard_map(body, mesh=mesh, in_specs=in_specs, out_specs=out_specs, check_vma=False)
```

profile of v0, /device:TPU:0, one launch (start us, length us, event | category | flops | bytes accessed | tf_op | source)
XLA Modules:
  0.0 48.2 jit_solution(11163739481269685602)
XLA Ops:
  0.0 6.0 %gather.1 = (bf16[520,128]{1,0:T(8,128)(2,1)S(1)}, bf16[520,128]{1,0:T(8,128)(2,1)S(1)}, bf16[520,128]{1,0:T(8,128)(2,1)S(1)}, bf16[520,128]{1,0:T(8,128)(2,1)S(...) custom-call(f32[2,8]{1,0:T(2,128)} %bitcast.13, ...), custom_call_target="tpu_custom_call" | custom-call | tf_op jit(solution)/shard_map/gather/pallas_call | solution.py:415
  6.0 4.1 %collective-permute-start.4 = (bf16[264,128]{1,0:T(8,128)(2,1)S(1)}, bf16[264,128]{1,0:T(8,128)(2,1)S(1)}, u32[]{:S(2)}, u32[]{:S(2)}) collective-permute-start(bf16[264,128]{1,0:T(8,128)(2,1)S(1)} %get-tuple-element.23), channel_id=1, source_target_pairs={{0,16},{4,20},{8,24},{12,28},{16,0},{20,4},{24,8},{28,12},{1,17},{... | collective-permute-start | bytes 202760 | tf_op jit(solution)/shard_map/ppermute | solution.py:393
  10.1 0.1 collective-permute-start.3
  10.2 1.8 %collective-permute-start = (bf16[520,128]{1,0:T(8,128)(2,1)S(1)}, bf16[520,128]{1,0:T(8,128)(2,1)S(1)}, u32[]{:S(2)}, u32[]{:S(2)}) collective-permute-start(bf16[520,128]{1,0:T(8,128)(2,1)S(1)} %get-tuple-element.19), channel_id=1, source_target_pairs={{0,4},{4,0},{8,12},{12,8},{16,20},{20,16},{24,28},{28,24},{1,5},{5... | collective-permute-start | bytes 399368 | tf_op jit(solution)/shard_map/ppermute | solution.py:393
  12.0 1.6 %collective-permute-start.1 = (bf16[520,128]{1,0:T(8,128)(2,1)S(1)}, bf16[520,128]{1,0:T(8,128)(2,1)S(1)}, u32[]{:S(2)}, u32[]{:S(2)}) collective-permute-start(bf16[520,128]{1,0:T(8,128)(2,1)S(1)} %get-tuple-element.20), channel_id=1, source_target_pairs={{0,8},{4,12},{8,0},{12,4},{16,24},{20,28},{24,16},{28,20},{1,9},{5... | collective-permute-start | bytes 399368 | tf_op jit(solution)/shard_map/ppermute | solution.py:393
  13.6 0.1 collective-permute-start.2
  13.7 0.4 collective-permute-done.4.rest_0_
  14.1 3.5 %collective-permute-start.5 = (bf16[264,128]{1,0:T(8,128)(2,1)S(1)}, bf16[264,128]{1,0:T(8,128)(2,1)S(1)}, u32[]{:S(2)}, u32[]{:S(2)}) collective-permute-start(bf16[264,128]{1,0:T(8,128)(2,1)S(1)} %get-tuple-element.24), channel_id=1, source_target_pairs={{0,20},{4,16},{8,28},{12,24},{16,4},{20,0},{24,12},{28,8},{1,21},{... | collective-permute-start | bytes 202760 | tf_op jit(solution)/shard_map/ppermute | solution.py:393
  17.5 2.5 %collective-permute-done.3.rest_4_ = bf16[520,128]{1,0:T(8,128)(2,1)S(1)} collective-permute-done((bf16[520,128]{1,0:T(8,128)(2,1)S(1)}, bf16[520,128]{1,0:T(8,128)(2,1)S(1)}, u32[]{:S(2)}, u32[]{:S(2)}) %collective-permute-start.3) | collective-permute-done | bytes 133152 | tf_op jit(solution)/shard_map/ppermute | solution.py:393
  20.0 1.8 %collective-permute-start.10 = (bf16[520,128]{1,0:T(8,128)(2,1)S(1)}, bf16[520,128]{1,0:T(8,128)(2,1)S(1)}, u32[]{:S(2)}, u32[]{:S(2)}) collective-permute-start(bf16[520,128]{1,0:T(8,128)(2,1)S(1)} %collective-permute-done.3.rest_4_), channel_id=1, source_target_pairs={{0,12},{4,8},{8,4},{12,0},{16,28},{20,24},{24,20},{28,16},{1,13},{... | collective-permute-start | bytes 399368 | tf_op jit(solution)/shard_map/ppermute | solution.py:393
  21.8 0.5 %collective-permute-done.5.rest_1_ = bf16[264,128]{1,0:T(8,128)(2,1)S(1)} collective-permute-done((bf16[264,128]{1,0:T(8,128)(2,1)S(1)}, bf16[264,128]{1,0:T(8,128)(2,1)S(1)}, u32[]{:S(2)}, u32[]{:S(2)}) %collective-permute-start.5) | collective-permute-done | bytes 67616 | tf_op jit(solution)/shard_map/ppermute | solution.py:393
  22.3 2.1 %collective-permute-start.8 = (bf16[520,128]{1,0:T(8,128)(2,1)S(1)}, bf16[520,128]{1,0:T(8,128)(2,1)S(1)}, u32[]{:S(2)}, u32[]{:S(2)}) collective-permute-start(bf16[520,128]{1,0:T(8,128)(2,1)S(1)} %collective-permute-done.3.rest_4_), channel_id=1, source_target_pairs={{0,4},{4,0},{8,12},{12,8},{16,20},{20,16},{24,28},{28,24},{1,5},{5... | collective-permute-start | bytes 399368 | tf_op jit(solution)/shard_map/ppermute | solution.py:393
  24.4 0.0 collective-permute-done.rest_1_
  24.4 2.8 %collective-permute-start.9 = (bf16[520,128]{1,0:T(8,128)(2,1)S(1)}, bf16[520,128]{1,0:T(8,128)(2,1)S(1)}, u32[]{:S(2)}, u32[]{:S(2)}) collective-permute-start(bf16[520,128]{1,0:T(8,128)(2,1)S(1)} %collective-permute-done.3.rest_4_), channel_id=1, source_target_pairs={{0,8},{4,12},{8,0},{12,4},{16,24},{20,28},{24,16},{28,20},{1,9},{5... | collective-permute-start | bytes 399368 | tf_op jit(solution)/shard_map/ppermute | solution.py:393
  27.2 0.0 collective-permute-done.1.rest_2_
  27.2 1.3 %collective-permute-start.6 = (bf16[264,128]{1,0:T(8,128)(2,1)S(1)}, bf16[264,128]{1,0:T(8,128)(2,1)S(1)}, u32[]{:S(2)}, u32[]{:S(2)}) collective-permute-start(bf16[264,128]{1,0:T(8,128)(2,1)S(1)} %get-tuple-element.25), channel_id=1, source_target_pairs={{0,24},{4,28},{8,16},{12,20},{16,8},{20,12},{24,0},{28,4},{1,25},{... | collective-permute-start | bytes 202760 | tf_op jit(solution)/shard_map/ppermute | solution.py:393
  28.5 0.0 collective-permute-done.2.rest_3_
  28.5 3.6 %collective-permute-start.7 = (bf16[264,128]{1,0:T(8,128)(2,1)S(1)}, bf16[264,128]{1,0:T(8,128)(2,1)S(1)}, u32[]{:S(2)}, u32[]{:S(2)}) collective-permute-start(bf16[264,128]{1,0:T(8,128)(2,1)S(1)} %get-tuple-element.26), channel_id=1, source_target_pairs={{0,28},{4,24},{8,20},{12,16},{16,12},{20,8},{24,4},{28,0},{1,29},{... | collective-permute-start | bytes 202760 | tf_op jit(solution)/shard_map/ppermute | solution.py:393
  32.1 2.1 %spectrum.1.early_ref = f32[1024,512]{1,0:T(8,128)S(1)} custom-call(bf16[520,128]{1,0:T(8,128)(2,1)S(1)} %get-tuple-element.18.rest_0_, bf16[520,128]{1,0:T(8,128)(2,1)S(1)} %collective-permute-done.rest_1_, bf16[520,128]{1,0:T(8,128)(2,1)S(1)} %collective-permute-done.1.rest_2_, bf16[520,128]{1,0:T(8,128)(2,1)S(1)} %collective-permute-done.2.rest_3_, ...), custom_call_target="tpu_custom_call" | custom-call | flops 1342177280 | bytes 4194304 | tf_op jit(solution)/shard_map/spectrum/pallas_call | solution.py:445
  34.2 0.0 collective-permute-done.6.rest_2_
  34.2 1.2 %collective-permute-done.7.rest_3_ = bf16[264,128]{1,0:T(8,128)(2,1)S(1)} collective-permute-done((bf16[264,128]{1,0:T(8,128)(2,1)S(1)}, bf16[264,128]{1,0:T(8,128)(2,1)S(1)}, u32[]{:S(2)}, u32[]{:S(2)}) %collective-permute-start.7) | collective-permute-done | bytes 67616 | tf_op jit(solution)/shard_map/ppermute | solution.py:393
  35.5 0.0 collective-permute-done.10.rest_6_
  35.5 0.0 collective-permute-done.8.rest_4_
  35.5 0.0 collective-permute-done.9.rest_5_
  35.5 3.4 %image.1 = (bf16[64,1024]{1,0:T(8,128)(2,1)S(1)}, bf16[64,1024]{1,0:T(8,128)(2,1)S(1)}, bf16[64,1024]{1,0:T(8,128)(2,1)S(1)}, bf16[64,1024]{1,0:T(8,128)(2,1)S(1)}) custom-call(bf16[256,512]{1,0:T(8,128)(2,1)S(1)} %copy-done, f32[1024,512]{1,0:T(8,128)S(1)} %spectrum.1.early_ref, bf16[264,128]{1,0:T(8,128)(2,1)S(1)} %collective-permute-done.4.rest_0_, ...), custom_call_target="tpu_custom_call" | custom-call | flops 1342177280 | bytes 4194304 | tf_op jit(solution)/shard_map/image/pallas_call | solution.py:457
  38.9 0.1 collective-permute-start.11
  39.0 1.6 %collective-permute-start.12 = (bf16[64,1024]{1,0:T(8,128)(2,1)S(1)}, bf16[64,1024]{1,0:T(8,128)(2,1)S(1)}, u32[]{:S(2)}, u32[]{:S(2)}) collective-permute-start(bf16[64,1024]{1,0:T(8,128)(2,1)S(1)} %get-tuple-element.29), channel_id=1, source_target_pairs={{0,2},{1,3},{2,0},{3,1},{4,6},{5,7},{6,4},{7,5},{8,10},{9,11},{10,... | collective-permute-start | bytes 393224 | tf_op jit(solution)/shard_map/ppermute | solution.py:393
  40.6 0.3 collective-permute-start.13
  40.9 0.0 collective-permute-done.11.refs_1_
  40.9 4.6 %collective-permute-done.12.refs_2_ = bf16[64,1024]{1,0:T(8,128)(2,1)S(1)} collective-permute-done((bf16[64,1024]{1,0:T(8,128)(2,1)S(1)}, bf16[64,1024]{1,0:T(8,128)(2,1)S(1)}, u32[]{:S(2)}, u32[]{:S(2)}) %collective-permute-start.12) | collective-permute-done | bytes 131104 | tf_op jit(solution)/shard_map/ppermute | solution.py:393
  45.4 1.7 %collective-permute-done.13.refs_3_ = bf16[64,1024]{1,0:T(8,128)(2,1)S(1)} collective-permute-done((bf16[64,1024]{1,0:T(8,128)(2,1)S(1)}, bf16[64,1024]{1,0:T(8,128)(2,1)S(1)}, u32[]{:S(2)}, u32[]{:S(2)}) %collective-permute-start.13) | collective-permute-done | bytes 131104 | tf_op jit(solution)/shard_map/ppermute | solution.py:393
  47.2 1.1 %finish.1 = f32[512,128]{1,0:T(8,128)} custom-call(bf16[64,1024]{1,0:T(8,128)(2,1)S(1)} %get-tuple-element.27.refs_0_, bf16[64,1024]{1,0:T(8,128)(2,1)S(1)} %collective-permute-done.11.refs_1_, bf16[64,1024]{1,0:T(8,128)(2,1)S(1)} %collective-permute-done.12.refs_2_, bf16[64,1024]{1,0:T(8,128)(2,1)S(1)} %collective-permute-done.13.refs_3_), custom_call_target="tpu_custom_call" | custom-call | tf_op jit(solution)/shard_map/finish/pallas_call | solution.py:468
  (2 shorter events, 0.0 us)
Async XLA Ops:
  0.0 35.5 %copy-start = (bf16[256,512]{1,0:T(8,128)(2,1)S(1)}, bf16[256,512]{1,0:T(8,128)(2,1)}, u32[]{:S(2)}) copy-start(bf16[256,512]{1,0:T(8,128)(2,1)} %constant.2.clone.table_ref) | copy-start | bytes 786436
  6.0 8.1 %collective-permute-start.4 = (bf16[264,128]{1,0:T(8,128)(2,1)S(1)}, bf16[264,128]{1,0:T(8,128)(2,1)S(1)}, u32[]{:S(2)}, u32[]{:S(2)}) collective-permute-start(bf16[264,128]{1,0:T(8,128)(2,1)S(1)} %get-tuple-element.23), channel_id=1, source_target_pairs={{0,16},{4,20},{8,24},{12,28},{16,0},{20,4},{24,8},{28,12},{1,17},{... | collective-permute-start | bytes 202760 | tf_op jit(solution)/shard_map/ppermute | solution.py:393
  10.1 9.9 %collective-permute-start.3 = (bf16[520,128]{1,0:T(8,128)(2,1)S(1)}, bf16[520,128]{1,0:T(8,128)(2,1)S(1)}, u32[]{:S(2)}, u32[]{:S(2)}) collective-permute-start(bf16[520,128]{1,0:T(8,128)(2,1)S(1)} %get-tuple-element.22), channel_id=1, source_target_pairs={{0,16},{4,20},{8,24},{12,28},{16,0},{20,4},{24,8},{28,12},{1,17},{... | collective-permute-start | bytes 399368 | tf_op jit(solution)/shard_map/ppermute | solution.py:393
  10.2 14.2 %collective-permute-start = (bf16[520,128]{1,0:T(8,128)(2,1)S(1)}, bf16[520,128]{1,0:T(8,128)(2,1)S(1)}, u32[]{:S(2)}, u32[]{:S(2)}) collective-permute-start(bf16[520,128]{1,0:T(8,128)(2,1)S(1)} %get-tuple-element.19), channel_id=1, source_target_pairs={{0,4},{4,0},{8,12},{12,8},{16,20},{20,16},{24,28},{28,24},{1,5},{5... | collective-permute-start | bytes 399368 | tf_op jit(solution)/shard_map/ppermute | solution.py:393
  12.0 15.2 %collective-permute-start.1 = (bf16[520,128]{1,0:T(8,128)(2,1)S(1)}, bf16[520,128]{1,0:T(8,128)(2,1)S(1)}, u32[]{:S(2)}, u32[]{:S(2)}) collective-permute-start(bf16[520,128]{1,0:T(8,128)(2,1)S(1)} %get-tuple-element.20), channel_id=1, source_target_pairs={{0,8},{4,12},{8,0},{12,4},{16,24},{20,28},{24,16},{28,20},{1,9},{5... | collective-permute-start | bytes 399368 | tf_op jit(solution)/shard_map/ppermute | solution.py:393
  13.6 14.9 %collective-permute-start.2 = (bf16[520,128]{1,0:T(8,128)(2,1)S(1)}, bf16[520,128]{1,0:T(8,128)(2,1)S(1)}, u32[]{:S(2)}, u32[]{:S(2)}) collective-permute-start(bf16[520,128]{1,0:T(8,128)(2,1)S(1)} %get-tuple-element.21), channel_id=1, source_target_pairs={{0,12},{4,8},{8,4},{12,0},{16,28},{20,24},{24,20},{28,16},{1,13},{... | collective-permute-start | bytes 399368 | tf_op jit(solution)/shard_map/ppermute | solution.py:393
  14.1 8.2 %collective-permute-start.5 = (bf16[264,128]{1,0:T(8,128)(2,1)S(1)}, bf16[264,128]{1,0:T(8,128)(2,1)S(1)}, u32[]{:S(2)}, u32[]{:S(2)}) collective-permute-start(bf16[264,128]{1,0:T(8,128)(2,1)S(1)} %get-tuple-element.24), channel_id=1, source_target_pairs={{0,20},{4,16},{8,28},{12,24},{16,4},{20,0},{24,12},{28,8},{1,21},{... | collective-permute-start | bytes 202760 | tf_op jit(solution)/shard_map/ppermute | solution.py:393
  20.0 15.5 %collective-permute-start.10 = (bf16[520,128]{1,0:T(8,128)(2,1)S(1)}, bf16[520,128]{1,0:T(8,128)(2,1)S(1)}, u32[]{:S(2)}, u32[]{:S(2)}) collective-permute-start(bf16[520,128]{1,0:T(8,128)(2,1)S(1)} %collective-permute-done.3.rest_4_), channel_id=1, source_target_pairs={{0,12},{4,8},{8,4},{12,0},{16,28},{20,24},{24,20},{28,16},{1,13},{... | collective-permute-start | bytes 399368 | tf_op jit(solution)/shard_map/ppermute | solution.py:393
  22.3 13.2 %collective-permute-start.8 = (bf16[520,128]{1,0:T(8,128)(2,1)S(1)}, bf16[520,128]{1,0:T(8,128)(2,1)S(1)}, u32[]{:S(2)}, u32[]{:S(2)}) collective-permute-start(bf16[520,128]{1,0:T(8,128)(2,1)S(1)} %collective-permute-done.3.rest_4_), channel_id=1, source_target_pairs={{0,4},{4,0},{8,12},{12,8},{16,20},{20,16},{24,28},{28,24},{1,5},{5... | collective-permute-start | bytes 399368 | tf_op jit(solution)/shard_map/ppermute | solution.py:393
  24.4 11.1 %collective-permute-start.9 = (bf16[520,128]{1,0:T(8,128)(2,1)S(1)}, bf16[520,128]{1,0:T(8,128)(2,1)S(1)}, u32[]{:S(2)}, u32[]{:S(2)}) collective-permute-start(bf16[520,128]{1,0:T(8,128)(2,1)S(1)} %collective-permute-done.3.rest_4_), channel_id=1, source_target_pairs={{0,8},{4,12},{8,0},{12,4},{16,24},{20,28},{24,16},{28,20},{1,9},{5... | collective-permute-start | bytes 399368 | tf_op jit(solution)/shard_map/ppermute | solution.py:393
  27.2 7.0 %collective-permute-start.6 = (bf16[264,128]{1,0:T(8,128)(2,1)S(1)}, bf16[264,128]{1,0:T(8,128)(2,1)S(1)}, u32[]{:S(2)}, u32[]{:S(2)}) collective-permute-start(bf16[264,128]{1,0:T(8,128)(2,1)S(1)} %get-tuple-element.25), channel_id=1, source_target_pairs={{0,24},{4,28},{8,16},{12,20},{16,8},{20,12},{24,0},{28,4},{1,25},{... | collective-permute-start | bytes 202760 | tf_op jit(solution)/shard_map/ppermute | solution.py:393
  28.5 7.0 %collective-permute-start.7 = (bf16[264,128]{1,0:T(8,128)(2,1)S(1)}, bf16[264,128]{1,0:T(8,128)(2,1)S(1)}, u32[]{:S(2)}, u32[]{:S(2)}) collective-permute-start(bf16[264,128]{1,0:T(8,128)(2,1)S(1)} %get-tuple-element.26), channel_id=1, source_target_pairs={{0,28},{4,24},{8,20},{12,16},{16,12},{20,8},{24,4},{28,0},{1,29},{... | collective-permute-start | bytes 202760 | tf_op jit(solution)/shard_map/ppermute | solution.py:393
  38.9 1.9 %collective-permute-start.11 = (bf16[64,1024]{1,0:T(8,128)(2,1)S(1)}, bf16[64,1024]{1,0:T(8,128)(2,1)S(1)}, u32[]{:S(2)}, u32[]{:S(2)}) collective-permute-start(bf16[64,1024]{1,0:T(8,128)(2,1)S(1)} %get-tuple-element.28), channel_id=1, source_target_pairs={{0,1},{1,0},{2,3},{3,2},{4,5},{5,4},{6,7},{7,6},{8,9},{9,8},{10,11... | collective-permute-start | bytes 393224 | tf_op jit(solution)/shard_map/ppermute | solution.py:393
  39.0 6.4 %collective-permute-start.12 = (bf16[64,1024]{1,0:T(8,128)(2,1)S(1)}, bf16[64,1024]{1,0:T(8,128)(2,1)S(1)}, u32[]{:S(2)}, u32[]{:S(2)}) collective-permute-start(bf16[64,1024]{1,0:T(8,128)(2,1)S(1)} %get-tuple-element.29), channel_id=1, source_target_pairs={{0,2},{1,3},{2,0},{3,1},{4,6},{5,7},{6,4},{7,5},{8,10},{9,11},{10,... | collective-permute-start | bytes 393224 | tf_op jit(solution)/shard_map/ppermute | solution.py:393
  40.6 6.6 %collective-permute-start.13 = (bf16[64,1024]{1,0:T(8,128)(2,1)S(1)}, bf16[64,1024]{1,0:T(8,128)(2,1)S(1)}, u32[]{:S(2)}, u32[]{:S(2)}) collective-permute-start(bf16[64,1024]{1,0:T(8,128)(2,1)S(1)} %get-tuple-element.30), channel_id=1, source_target_pairs={{0,3},{1,2},{2,1},{3,0},{4,7},{5,6},{6,5},{7,4},{8,11},{9,10},{10,... | collective-permute-start | bytes 393224 | tf_op jit(solution)/shard_map/ppermute | solution.py:393
where the time goes:
time: 48.4 us; the launch traced here: 48.2 us
  starting transfers between devices  24.6 us (51%)
  Pallas kernels  12.6 us (26%)
  waiting for transfers between devices  10.9 us (23%)
    ppermute x14, starting transfers between devices, swap(): return lax.ppermute(piece, axis, [(i, i ^ distance) for i in range(count)])  24.6 us
    ppermute x14, waiting for transfers between devices, swap(): return lax.ppermute(piece, axis, [(i, i ^ distance) for i in range(count)])  10.9 us
    pallas_call x1, Pallas kernels, packed_shards(): pl.pallas_call(functools.partial(gather_kernel, peers, sizes), out_shape=...  6 us
    pallas_call x1, Pallas kernels, packed_shards(): pl.pallas_call(functools.partial(image_kernel, late_sizes, near, groups),...  3.44 us
    pallas_call x1, Pallas kernels, packed_shards(): pl.pallas_call(functools.partial(spectrum_kernel, early_sizes, near), out...  2.11 us
    pallas_call x1, Pallas kernels, packed_shards(): pl.pallas_call(functools.partial(finish_kernel, groups), out_shape=jax.Sh...  1.07 us
  transfers between devices with their start and end apart: 14, of which 6 were waited for; matrix products, arithmetic and copies ran while one was open for 0% of the time, Pallas kernels for 4%

commit v1 on v0

--- a/solution.py
+++ b/solution.py
@@ -189,7 +189,7 @@
     zero_row = jnp.zeros_like(l_row)
     columns = jnp.concatenate([l_row, m_row, d_row, plane_row] + [zero_row] * 4, axis=0).T
 
-    near, capacity, few, slots = peers // 2, sizes[0], sizes[peers // 2], sum(sizes)
+    near, capacity, few, slots = peers // 2, sizes[0], sizes[peers // 2], LANES * len(sizes)
     relative = facet ^ lax.axis_index("facet")
     lanes = lax.broadcasted_iota(jnp.int32, (tiles, tiles), 1)
     earlier = (lax.broadcasted_iota(jnp.int32, (tiles, tiles), 0) < lanes).astype(jnp.float32).astype(jnp.bfloat16)
@@ -199,9 +199,7 @@
     rank = jnp.sum(jnp.where(hits, before, 0.0), axis=0, keepdims=True).astype(jnp.int32)
     passed = jnp.where(facets >= near, jnp.maximum(before - few, 0.0), 0.0)
     passed = jnp.sum(passed, axis=0, keepdims=True).astype(jnp.int32)
-    direct = near * capacity + (relative - near) * few + rank
-    slot = jnp.where(rank < few, direct, near * (capacity + few) + passed)
-    slot = jnp.where(relative < near, relative * capacity + rank, slot)
+    slot = jnp.where((relative < near) | (rank < few), relative * capacity + rank, peers * capacity + passed)
 
     patches = []
     for h in range(2):
@@ -245,24 +243,26 @@
     labels = [block_u, block_v, facet.astype(jnp.float32)] + [zero_row] * (SUBLANES - 3)
     labels = jnp.concatenate(labels, axis=0).astype(jnp.bfloat16)
     labels = lax.dot_general(labels, placing, (((1,), (1,)), ((), ())), preferred_element_type=jnp.float32)
-    lane = lax.broadcasted_iota(jnp.int32, (SUBLANES, LANES), 1)
-    start = 0
-    for ref, size in zip(out_refs, sizes):
+    labels = labels.astype(jnp.bfloat16)
+    for i, (ref, size) in enumerate(zip(out_refs, sizes)):
+        start = i * LANES
         for j in range(2 * cells // LANES):
             ref[j * size : (j + 1) * size, :] = placed[start : start + size, j * LANES : (j + 1) * LANES]
-        tile = start // LANES * LANES
-        inside = (lane >= start - tile) & (lane < start - tile + size)
-        ref[2 * cells // LANES * size :, :] = jnp.where(inside, labels[:, tile : tile + LANES], 0.0).astype(jnp.bfloat16)
-        start += size
+        ref[2 * cells // LANES * size :, :] = labels[:, start : start + LANES]
+
+
+def padded(sizes):
+    return -(-sum(sizes) // LANES) * LANES
 
 
 def load_patches(in_refs, sizes, patch_buf):
     cells = PSIDE * PSIDE
     half_tiles = cells // LANES
+    slots = padded(sizes)
     start = 0
     for ref, size in zip(in_refs, sizes):
         rows = slice(start, start + size)
-        below = slice(sum(sizes) + start, sum(sizes) + start + size)
+        below = slice(slots + start, slots + start + size)
         for j in range(half_tiles):
             left = slice(j * LANES, (j + 1) * LANES)
             right = slice(cells + j * LANES, cells + (j + 1) * LANES)
@@ -273,22 +273,31 @@
             patch_buf[below, left] = -imag
             patch_buf[below, right] = real
         start += size
+    if start < slots:
+        for first in (0, slots):
+            patch_buf[first + start : first + slots, :] = jnp.zeros((slots - start, 2 * cells), jnp.bfloat16)
 
 
 def cell_phases(in_refs, sizes, direct):
-    labels, start = [], 0
+    slots = padded(sizes)
+    labels = [jnp.zeros((SUBLANES, LANES), jnp.float32) for _ in range(slots // LANES)]
+    lane = lax.broadcasted_iota(jnp.int32, (SUBLANES, LANES), 1)
+    start = 0
     for ref, size in zip(in_refs, sizes):
         here = ref[2 * PSIDE * PSIDE // LANES * size :, :].astype(jnp.float32)
-        if start % LANES:
-            labels[-1] = labels[-1] + here
-        else:
-            labels.append(here)
+        tile, shift = divmod(start, LANES)
+        if shift:
+            here = pltpu.roll(here, shift, 1)
+            if shift + size > LANES:
+                labels[tile + 1] = jnp.where(lane < shift, here, 0.0)
+            here = jnp.where(lane >= shift, here, 0.0)
+        labels[tile] = labels[tile] + here
         start += size
     labels = jnp.concatenate(labels, axis=1)
-    lane = lax.broadcasted_iota(jnp.int32, (1, start), 1)
+    lane = lax.broadcasted_iota(jnp.int32, (1, slots), 1)
     mine = labels[2:3] == lax.axis_index("facet").astype(jnp.float32)
     mine = jnp.where(mine | (lane < sum(sizes[:direct])), 1.0, 0.0)
-    index = lax.broadcasted_iota(jnp.int32, (NBLK, start), 0).astype(jnp.float32) * (1.0 / NBLK)
+    index = lax.broadcasted_iota(jnp.int32, (NBLK, slots), 0).astype(jnp.float32) * (1.0 / NBLK)
     cos_u, sin_u = cos_sin_turns(index * labels[0:1])
     return (cos_u * mine, sin_u * mine) + cos_sin_turns(index * labels[1:2])
 
@@ -308,7 +317,7 @@
 
 def spectrum_kernel(sizes, direct, *rest):
     count = len(sizes)
-    in_refs, out_ref, (phases_buf, patch_buf) = rest[:count], rest[count], rest[count + 1 :]
+    in_refs, (out_ref, turn_ref, phases_buf, patch_buf) = rest[:count], rest[count:]
     load_patches(in_refs, sizes, patch_buf)
     phases = cell_phases(in_refs, sizes, direct)
     width = PER_CHUNK * NBLK
@@ -319,8 +328,19 @@
             buf[...], patch_buf[...], preferred_element_type=jnp.float32
         )
 
-
-def image_kernel(sizes, direct, groups, table_ref, early_ref, *rest):
+    cells = PSIDE * PSIDE
+    lane = lax.broadcasted_iota(jnp.int32, (NBLK, cells), 1)
+    row = lax.broadcasted_iota(jnp.int32, (NBLK, cells), 0)
+    cos_u, sin_u = cos_sin_turns((row * (lane // PSIDE)).astype(jnp.float32) * (1.0 / GRID))
+    cos_v, sin_v = cos_sin_turns((row * (lane % PSIDE)).astype(jnp.float32) * (1.0 / GRID))
+    for j in range(NBLK):
+        rows = slice(j * NBLK, (j + 1) * NBLK)
+        cu, su = cos_u[j : j + 1], sin_u[j : j + 1]
+        turn_ref[rows, :cells] = cu * cos_v - su * sin_v
+        turn_ref[rows, cells:] = cu * sin_v + su * cos_v
+
+
+def image_kernel(sizes, direct, groups, table_ref, early_ref, turn_ref, *rest):
     count = len(sizes)
     in_refs, out_refs = rest[:count], rest[count : count + groups]
     phases_buf, patch_buf, table_buf = rest[count + groups :]
@@ -332,27 +352,15 @@
         table_buf[s * share : (s + 1) * share, :] = table_ref[pl.ds(start, share), :]
     phases = cell_phases(in_refs, sizes, direct)
 
-    lane = lax.broadcasted_iota(jnp.int32, (NBLK, cells), 1)
-    row = lax.broadcasted_iota(jnp.int32, (NBLK, cells), 0)
-    patch_u, patch_v = lane // PSIDE, lane % PSIDE
-    twid_u = cos_sin_turns((row * patch_u).astype(jnp.float32) * (1.0 / GRID))
-    twid_v = cos_sin_turns((row * patch_v).astype(jnp.float32) * (1.0 / GRID))
-
     width = PER_CHUNK * NBLK
     for chunk in range(NBLK // PER_CHUNK):
         buf = phases_buf.at[chunk % 2]
         fill_phases(buf, range(chunk * PER_CHUNK, (chunk + 1) * PER_CHUNK), phases)
         here = slice(chunk * width, (chunk + 1) * width)
         spectrum = early_ref[here, :] + jnp.dot(buf[...], patch_buf[...], preferred_element_type=jnp.float32)
-        turned = []
-        for i in range(PER_CHUNK):
-            j = chunk * PER_CHUNK + i
-            rows = slice(i * NBLK, (i + 1) * NBLK)
-            real, imag = spectrum[rows, :cells], spectrum[rows, cells:]
-            tr = twid_u[0][j : j + 1] * twid_v[0] - twid_u[1][j : j + 1] * twid_v[1]
-            ti = twid_u[0][j : j + 1] * twid_v[1] + twid_u[1][j : j + 1] * twid_v[0]
-            turned.append(jnp.concatenate([real * tr - imag * ti, real * ti + imag * tr], axis=1).astype(jnp.bfloat16))
-        turned = jnp.concatenate(turned, axis=0)
+        real, imag = spectrum[:, :cells], spectrum[:, cells:]
+        cosine, sine = turn_ref[here, :cells], turn_ref[here, cells:]
+        turned = jnp.concatenate([real * cosine - imag * sine, real * sine + imag * cosine], axis=1).astype(jnp.bfloat16)
         image = lax.dot_general(
             table_buf[...], turned, (((1,), (1,)), ((), ())), preferred_element_type=jnp.float32
         ).astype(jnp.bfloat16)
@@ -393,13 +401,22 @@
     return lax.ppermute(piece, axis, [(i, i ^ distance) for i in range(count)])
 
 
+def overflow_slots(tiles, capacity, few, facets):
+    full = min(facets, tiles // capacity)
+    most = full * (capacity - few)
+    if full < facets:
+        most += max(0, tiles - full * capacity - few)
+    return -(-most // 16) * 16
+
+
 def packed_shards(visibilities, uvw, facet_of, plane_of, cell_of, kernels, centers):
     peers, groups = lax.axis_size("facet"), lax.axis_size("freq")
     tiles = visibilities.shape[1]
     capacity = 4 * tiles // peers
     planes, _, depth, cells = kernels.shape
     near = peers // 2
-    sizes = [capacity] * near + [capacity // 2] * near + [tiles // 2]
+    few = 5 * capacity // 8
+    sizes = [capacity] * near + [few] * near + [overflow_slots(tiles, capacity, few, near)]
     payloads = [jax.ShapeDtypeStruct((2 * cells // LANES * size + SUBLANES, LANES), jnp.bfloat16) for size in sizes]
     lanes = depth // LANES
     vis_rows = visibilities[0].reshape(tiles, 2, lanes, LANES).transpose(0, 2, 1, 3).reshape(-1, LANES)
@@ -441,29 +458,29 @@
         ]
         return buffers, pl.CostEstimate(flops=8 * points * slots * cells, bytes_accessed=4 << 20, transcendentals=0)
 
-    buffers, cost = buffers_and_cost(sum(early_sizes))
-    spectrum = pl.pallas_call(
+    buffers, cost = buffers_and_cost(padded(early_sizes))
+    spectrum, turns = pl.pallas_call(
         functools.partial(spectrum_kernel, early_sizes, near),
-        out_shape=jax.ShapeDtypeStruct((points, 2 * cells), jnp.float32),
+        out_shape=[jax.ShapeDtypeStruct((points, 2 * cells), jnp.float32)] * 2,
         in_specs=[VMEM] * len(early),
-        out_specs=VMEM,
+        out_specs=[VMEM] * 2,
         scratch_shapes=buffers,
         compiler_params=compiler_params(40),
         cost_estimate=cost,
         name="spectrum",
     )(*early)
-    buffers, cost = buffers_and_cost(sum(late_sizes))
+    buffers, cost = buffers_and_cost(padded(late_sizes))
     image = jax.ShapeDtypeStruct((share, points), jnp.bfloat16)
     images = pl.pallas_call(
         functools.partial(image_kernel, late_sizes, near, groups),
         out_shape=[image] * groups,
-        in_specs=[VMEM] * (2 + len(late)),
+        in_specs=[VMEM] * (3 + len(late)),
         out_specs=[VMEM] * groups,
         scratch_shapes=buffers + [pltpu.VMEM((cells, 2 * cells), jnp.bfloat16)],
         compiler_params=compiler_params(40),
         cost_estimate=cost,
         name="image",
-    )(jnp.asarray(patch_table(), jnp.bfloat16), spectrum, *late)
+    )(jnp.asarray(patch_table(), jnp.bfloat16), spectrum, turns, *late)
     summed = [images[0]] + [swap(images[s], "freq", s) for s in range(1, groups)]
     facet_image = pl.pallas_call(
         functools.partial(finish_kernel, groups),

time: 48.4 us -> 50.3 us (1.039)
  waiting for transfers between devices: 10.9 us -> 17.1 us
  starting transfers between devices: 24.6 us -> 20.1 us
    ppermute x14, waiting for transfers between devices: 10.9 us -> 17.1 us  [swap(): return lax.ppermute(piece, axis, [(i, i ^ distance) for i in range(count)])]
    ppermute x14, starting transfers between devices: 24.6 us -> 20.1 us  [swap(): return lax.ppermute(piece, axis, [(i, i ^ distance) for i in range(count)])]
  transfers between devices with their start and end apart: 14 -> 14, of which waited for: 6 -> 7; matrix products, arithmetic and copies ran while one was open for 0% -> 0% of each run, Pallas kernels for 4% -> 5%
where the time goes in v1:
time: 50.3 us; the launch traced here: 50.1 us
  starting transfers between devices  20.1 us (40%)
  waiting for transfers between devices  17.1 us (34%)
  Pallas kernels  12.9 us (26%)
    ppermute x14, starting transfers between devices, swap(): return lax.ppermute(piece, axis, [(i, i ^ distance) for i in range(count)])  20.1 us
    ppermute x14, waiting for transfers between devices, swap(): return lax.ppermute(piece, axis, [(i, i ^ distance) for i in range(count)])  17.1 us
    pallas_call x1, Pallas kernels, packed_shards(): pl.pallas_call(functools.partial(gather_kernel, peers, sizes), out_shape=...  6.06 us
    pallas_call x1, Pallas kernels, packed_shards(): pl.pallas_call(functools.partial(image_kernel, late_sizes, near, groups),...  3.32 us
    pallas_call x1, Pallas kernels, packed_shards(): pl.pallas_call(functools.partial(spectrum_kernel, early_sizes, near), out...  2.43 us
    pallas_call x1, Pallas kernels, packed_shards(): pl.pallas_call(functools.partial(finish_kernel, groups), out_shape=jax.Sh...  1.07 us
  transfers between devices with their start and end apart: 14, of which 7 were waited for; matrix products, arithmetic and copies ran while one was open for 0% of the time, Pallas kernels for 5%

profile of v1, /device:TPU:0, one launch (start us, length us, event | category | flops | bytes accessed | tf_op | source)
XLA Modules:
  0.0 50.1 jit_solution(11902951952577857572)
XLA Ops:
  0.0 6.1 %gather.1 = (bf16[520,128]{1,0:T(8,128)(2,1)S(1)}, bf16[520,128]{1,0:T(8,128)(2,1)S(1)}, bf16[520,128]{1,0:T(8,128)(2,1)S(1)}, bf16[520,128]{1,0:T(8,128)(2,1)S(...) custom-call(f32[2,8]{1,0:T(2,128)} %bitcast.13, ...), custom_call_target="tpu_custom_call" | custom-call | tf_op jit(solution)/shard_map/gather/pallas_call | solution.py:432
  6.1 4.1 %collective-permute-start.4 = (bf16[328,128]{1,0:T(8,128)(2,1)S(1)}, bf16[328,128]{1,0:T(8,128)(2,1)S(1)}, u32[]{:S(2)}, u32[]{:S(2)}) collective-permute-start(bf16[328,128]{1,0:T(8,128)(2,1)S(1)} %get-tuple-element.27), channel_id=1, source_target_pairs={{0,16},{4,20},{8,24},{12,28},{16,0},{20,4},{24,8},{28,12},{1,17},{... | collective-permute-start | bytes 251912 | tf_op jit(solution)/shard_map/ppermute | solution.py:401
  10.2 1.5 %collective-permute-start = (bf16[520,128]{1,0:T(8,128)(2,1)S(1)}, bf16[520,128]{1,0:T(8,128)(2,1)S(1)}, u32[]{:S(2)}, u32[]{:S(2)}) collective-permute-start(bf16[520,128]{1,0:T(8,128)(2,1)S(1)} %get-tuple-element.21), channel_id=1, source_target_pairs={{0,4},{4,0},{8,12},{12,8},{16,20},{20,16},{24,28},{28,24},{1,5},{5... | collective-permute-start | bytes 399368 | tf_op jit(solution)/shard_map/ppermute | solution.py:401
  11.7 1.6 %collective-permute-start.1 = (bf16[520,128]{1,0:T(8,128)(2,1)S(1)}, bf16[520,128]{1,0:T(8,128)(2,1)S(1)}, u32[]{:S(2)}, u32[]{:S(2)}) collective-permute-start(bf16[520,128]{1,0:T(8,128)(2,1)S(1)} %get-tuple-element.22), channel_id=1, source_target_pairs={{0,8},{4,12},{8,0},{12,4},{16,24},{20,28},{24,16},{28,20},{1,9},{5... | collective-permute-start | bytes 399368 | tf_op jit(solution)/shard_map/ppermute | solution.py:401
  13.3 0.4 collective-permute-start.2
  13.7 0.1 collective-permute-start.3
  13.8 0.6 %collective-permute-done.4.rest_0_ = bf16[328,128]{1,0:T(8,128)(2,1)S(1)} collective-permute-done((bf16[328,128]{1,0:T(8,128)(2,1)S(1)}, bf16[328,128]{1,0:T(8,128)(2,1)S(1)}, u32[]{:S(2)}, u32[]{:S(2)}) %collective-permute-start.4) | collective-permute-done | bytes 84000 | tf_op jit(solution)/shard_map/ppermute | solution.py:401
  14.4 3.2 %collective-permute-start.5 = (bf16[328,128]{1,0:T(8,128)(2,1)S(1)}, bf16[328,128]{1,0:T(8,128)(2,1)S(1)}, u32[]{:S(2)}, u32[]{:S(2)}) collective-permute-start(bf16[328,128]{1,0:T(8,128)(2,1)S(1)} %get-tuple-element.28), channel_id=1, source_target_pairs={{0,20},{4,16},{8,28},{12,24},{16,4},{20,0},{24,12},{28,8},{1,21},{... | collective-permute-start | bytes 251912 | tf_op jit(solution)/shard_map/ppermute | solution.py:401
  17.6 7.5 %collective-permute-done.5.rest_1_ = bf16[328,128]{1,0:T(8,128)(2,1)S(1)} collective-permute-done((bf16[328,128]{1,0:T(8,128)(2,1)S(1)}, bf16[328,128]{1,0:T(8,128)(2,1)S(1)}, u32[]{:S(2)}, u32[]{:S(2)}) %collective-permute-start.5) | collective-permute-done | bytes 84000 | tf_op jit(solution)/shard_map/ppermute | solution.py:401
  25.0 2.9 %collective-permute-start.6 = (bf16[328,128]{1,0:T(8,128)(2,1)S(1)}, bf16[328,128]{1,0:T(8,128)(2,1)S(1)}, u32[]{:S(2)}, u32[]{:S(2)}) collective-permute-start(bf16[328,128]{1,0:T(8,128)(2,1)S(1)} %get-tuple-element.29), channel_id=1, source_target_pairs={{0,24},{4,28},{8,16},{12,20},{16,8},{20,12},{24,0},{28,4},{1,25},{... | collective-permute-start | bytes 251912 | tf_op jit(solution)/shard_map/ppermute | solution.py:401
  27.9 0.0 collective-permute-done.3.rest_4_
  27.9 0.9 %collective-permute-start.7 = (bf16[328,128]{1,0:T(8,128)(2,1)S(1)}, bf16[328,128]{1,0:T(8,128)(2,1)S(1)}, u32[]{:S(2)}, u32[]{:S(2)}) collective-permute-start(bf16[328,128]{1,0:T(8,128)(2,1)S(1)} %get-tuple-element.30), channel_id=1, source_target_pairs={{0,28},{4,24},{8,20},{12,16},{16,12},{20,8},{24,4},{28,0},{1,29},{... | collective-permute-start | bytes 251912 | tf_op jit(solution)/shard_map/ppermute | solution.py:401
  28.8 0.0 collective-permute-done.rest_1_
  28.8 0.0 collective-permute-start.10
  28.8 0.0 collective-permute-done.1.rest_2_
  28.8 1.6 %collective-permute-start.8 = (bf16[392,128]{1,0:T(8,128)(2,1)S(1)}, bf16[392,128]{1,0:T(8,128)(2,1)S(1)}, u32[]{:S(2)}, u32[]{:S(2)}) collective-permute-start(bf16[392,128]{1,0:T(8,128)(2,1)S(1)} %collective-permute-done.3.rest_4_), channel_id=1, source_target_pairs={{0,4},{4,0},{8,12},{12,8},{16,20},{20,16},{24,28},{28,24},{1,5},{5... | collective-permute-start | bytes 301064 | tf_op jit(solution)/shard_map/ppermute | solution.py:401
  30.4 0.0 collective-permute-done.2.rest_3_
  30.4 1.9 %collective-permute-start.9 = (bf16[392,128]{1,0:T(8,128)(2,1)S(1)}, bf16[392,128]{1,0:T(8,128)(2,1)S(1)}, u32[]{:S(2)}, u32[]{:S(2)}) collective-permute-start(bf16[392,128]{1,0:T(8,128)(2,1)S(1)} %collective-permute-done.3.rest_4_), channel_id=1, source_target_pairs={{0,8},{4,12},{8,0},{12,4},{16,24},{20,28},{24,16},{28,20},{1,9},{5... | collective-permute-start | bytes 301064 | tf_op jit(solution)/shard_map/ppermute | solution.py:401
  32.3 2.4 %spectrum.1 = (f32[1024,512]{1,0:T(8,128)S(1)}, f32[1024,512]{1,0:T(8,128)S(1)}) custom-call(bf16[520,128]{1,0:T(8,128)(2,1)S(1)} %get-tuple-element.20.rest_0_, bf16[520,128]{1,0:T(8,128)(2,1)S(1)} %collective-permute-done.rest_1_, bf16[520,128]{1,0:T(8,128)(2,1)S(1)} %collective-permute-done.1.rest_2_, ...), custom_call_target="tpu_custom_call" | custom-call | flops 1342177280 | bytes 4194304 | tf_op jit(solution)/shard_map/spectrum/pallas_call | solution.py:462
  34.7 0.0 collective-permute-done.6.rest_2_
  34.8 0.7 %collective-permute-done.7.rest_3_ = bf16[328,128]{1,0:T(8,128)(2,1)S(1)} collective-permute-done((bf16[328,128]{1,0:T(8,128)(2,1)S(1)}, bf16[328,128]{1,0:T(8,128)(2,1)S(1)}, u32[]{:S(2)}, u32[]{:S(2)}) %collective-permute-start.7) | collective-permute-done | bytes 84000 | tf_op jit(solution)/shard_map/ppermute | solution.py:401
  35.4 1.0 %collective-permute-done.10.rest_6_ = bf16[392,128]{1,0:T(8,128)(2,1)S(1)} collective-permute-done((bf16[392,128]{1,0:T(8,128)(2,1)S(1)}, bf16[392,128]{1,0:T(8,128)(2,1)S(1)}, u32[]{:S(2)}, u32[]{:S(2)}) %collective-permute-start.10) | collective-permute-done | bytes 100384 | tf_op jit(solution)/shard_map/ppermute | solution.py:401
  36.4 0.0 collective-permute-done.8.rest_4_
  36.4 1.1 %collective-permute-done.9.rest_5_ = bf16[392,128]{1,0:T(8,128)(2,1)S(1)} collective-permute-done((bf16[392,128]{1,0:T(8,128)(2,1)S(1)}, bf16[392,128]{1,0:T(8,128)(2,1)S(1)}, u32[]{:S(2)}, u32[]{:S(2)}) %collective-permute-start.9) | collective-permute-done | bytes 100384 | tf_op jit(solution)/shard_map/ppermute | solution.py:401
  37.5 3.3 %image.1 = (bf16[64,1024]{1,0:T(8,128)(2,1)S(1)}, bf16[64,1024]{1,0:T(8,128)(2,1)S(1)}, bf16[64,1024]{1,0:T(8,128)(2,1)S(1)}, bf16[64,1024]{1,0:T(8,128)(2,1)S(1)}) custom-call(bf16[256,512]{1,0:T(8,128)(2,1)S(1)} %copy-done, f32[1024,512]{1,0:T(8,128)S(1)} %get-tuple-element.25.early_ref, f32[1024,512]{1,0:T(8,128)S(1)} %get-tuple-element.26.turn_ref, ...), custom_call_target="tpu_custom_call" | custom-call | flops 1342177280 | bytes 4194304 | tf_op jit(solution)/shard_map/image/pallas_call | solution.py:474
  40.8 0.1 collective-permute-start.11
  40.9 1.5 %collective-permute-start.12 = (bf16[64,1024]{1,0:T(8,128)(2,1)S(1)}, bf16[64,1024]{1,0:T(8,128)(2,1)S(1)}, u32[]{:S(2)}, u32[]{:S(2)}) collective-permute-start(bf16[64,1024]{1,0:T(8,128)(2,1)S(1)} %get-tuple-element.33), channel_id=1, source_target_pairs={{0,2},{1,3},{2,0},{3,1},{4,6},{5,7},{6,4},{7,5},{8,10},{9,11},{10,... | collective-permute-start | bytes 393224 | tf_op jit(solution)/shard_map/ppermute | solution.py:401
  42.5 0.3 collective-permute-start.13
  42.8 0.0 collective-permute-done.11.refs_1_
  42.8 4.6 %collective-permute-done.12.refs_2_ = bf16[64,1024]{1,0:T(8,128)(2,1)S(1)} collective-permute-done((bf16[64,1024]{1,0:T(8,128)(2,1)S(1)}, bf16[64,1024]{1,0:T(8,128)(2,1)S(1)}, u32[]{:S(2)}, u32[]{:S(2)}) %collective-permute-start.12) | collective-permute-done | bytes 131104 | tf_op jit(solution)/shard_map/ppermute | solution.py:401
  47.3 1.7 %collective-permute-done.13.refs_3_ = bf16[64,1024]{1,0:T(8,128)(2,1)S(1)} collective-permute-done((bf16[64,1024]{1,0:T(8,128)(2,1)S(1)}, bf16[64,1024]{1,0:T(8,128)(2,1)S(1)}, u32[]{:S(2)}, u32[]{:S(2)}) %collective-permute-start.13) | collective-permute-done | bytes 131104 | tf_op jit(solution)/shard_map/ppermute | solution.py:401
  49.1 1.1 %finish.1 = f32[512,128]{1,0:T(8,128)} custom-call(bf16[64,1024]{1,0:T(8,128)(2,1)S(1)} %get-tuple-element.31.refs_0_, bf16[64,1024]{1,0:T(8,128)(2,1)S(1)} %collective-permute-done.11.refs_1_, bf16[64,1024]{1,0:T(8,128)(2,1)S(1)} %collective-permute-done.12.refs_2_, bf16[64,1024]{1,0:T(8,128)(2,1)S(1)} %collective-permute-done.13.refs_3_), custom_call_target="tpu_custom_call" | custom-call | tf_op jit(solution)/shard_map/finish/pallas_call | solution.py:485
  (2 shorter events, 0.0 us)
Async XLA Ops:
  6.1 8.3 %collective-permute-start.4 = (bf16[328,128]{1,0:T(8,128)(2,1)S(1)}, bf16[328,128]{1,0:T(8,128)(2,1)S(1)}, u32[]{:S(2)}, u32[]{:S(2)}) collective-permute-start(bf16[328,128]{1,0:T(8,128)(2,1)S(1)} %get-tuple-element.27), channel_id=1, source_target_pairs={{0,16},{4,20},{8,24},{12,28},{16,0},{20,4},{24,8},{28,12},{1,17},{... | collective-permute-start | bytes 251912 | tf_op jit(solution)/shard_map/ppermute | solution.py:401
  10.2 18.6 %collective-permute-start = (bf16[520,128]{1,0:T(8,128)(2,1)S(1)}, bf16[520,128]{1,0:T(8,128)(2,1)S(1)}, u32[]{:S(2)}, u32[]{:S(2)}) collective-permute-start(bf16[520,128]{1,0:T(8,128)(2,1)S(1)} %get-tuple-element.21), channel_id=1, source_target_pairs={{0,4},{4,0},{8,12},{12,8},{16,20},{20,16},{24,28},{28,24},{1,5},{5... | collective-permute-start | bytes 399368 | tf_op jit(solution)/shard_map/ppermute | solution.py:401
  11.7 17.1 %collective-permute-start.1 = (bf16[520,128]{1,0:T(8,128)(2,1)S(1)}, bf16[520,128]{1,0:T(8,128)(2,1)S(1)}, u32[]{:S(2)}, u32[]{:S(2)}) collective-permute-start(bf16[520,128]{1,0:T(8,128)(2,1)S(1)} %get-tuple-element.22), channel_id=1, source_target_pairs={{0,8},{4,12},{8,0},{12,4},{16,24},{20,28},{24,16},{28,20},{1,9},{5... | collective-permute-start | bytes 399368 | tf_op jit(solution)/shard_map/ppermute | solution.py:401
  13.3 17.1 %collective-permute-start.2 = (bf16[520,128]{1,0:T(8,128)(2,1)S(1)}, bf16[520,128]{1,0:T(8,128)(2,1)S(1)}, u32[]{:S(2)}, u32[]{:S(2)}) collective-permute-start(bf16[520,128]{1,0:T(8,128)(2,1)S(1)} %get-tuple-element.23), channel_id=1, source_target_pairs={{0,12},{4,8},{8,4},{12,0},{16,28},{20,24},{24,20},{28,16},{1,13},{... | collective-permute-start | bytes 399368 | tf_op jit(solution)/shard_map/ppermute | solution.py:401
  13.7 14.2 %collective-permute-start.3 = (bf16[392,128]{1,0:T(8,128)(2,1)S(1)}, bf16[392,128]{1,0:T(8,128)(2,1)S(1)}, u32[]{:S(2)}, u32[]{:S(2)}) collective-permute-start(bf16[392,128]{1,0:T(8,128)(2,1)S(1)} %get-tuple-element.24), channel_id=1, source_target_pairs={{0,16},{4,20},{8,24},{12,28},{16,0},{20,4},{24,8},{28,12},{1,17},{... | collective-permute-start | bytes 301064 | tf_op jit(solution)/shard_map/ppermute | solution.py:401
  14.4 10.7 %collective-permute-start.5 = (bf16[328,128]{1,0:T(8,128)(2,1)S(1)}, bf16[328,128]{1,0:T(8,128)(2,1)S(1)}, u32[]{:S(2)}, u32[]{:S(2)}) collective-permute-start(bf16[328,128]{1,0:T(8,128)(2,1)S(1)} %get-tuple-element.28), channel_id=1, source_target_pairs={{0,20},{4,16},{8,28},{12,24},{16,4},{20,0},{24,12},{28,8},{1,21},{... | collective-permute-start | bytes 251912 | tf_op jit(solution)/shard_map/ppermute | solution.py:401
  25.0 9.7 %collective-permute-start.6 = (bf16[328,128]{1,0:T(8,128)(2,1)S(1)}, bf16[328,128]{1,0:T(8,128)(2,1)S(1)}, u32[]{:S(2)}, u32[]{:S(2)}) collective-permute-start(bf16[328,128]{1,0:T(8,128)(2,1)S(1)} %get-tuple-element.29), channel_id=1, source_target_pairs={{0,24},{4,28},{8,16},{12,20},{16,8},{20,12},{24,0},{28,4},{1,25},{... | collective-permute-start | bytes 251912 | tf_op jit(solution)/shard_map/ppermute | solution.py:401
  27.9 7.5 %collective-permute-start.7 = (bf16[328,128]{1,0:T(8,128)(2,1)S(1)}, bf16[328,128]{1,0:T(8,128)(2,1)S(1)}, u32[]{:S(2)}, u32[]{:S(2)}) collective-permute-start(bf16[328,128]{1,0:T(8,128)(2,1)S(1)} %get-tuple-element.30), channel_id=1, source_target_pairs={{0,28},{4,24},{8,20},{12,16},{16,12},{20,8},{24,4},{28,0},{1,29},{... | collective-permute-start | bytes 251912 | tf_op jit(solution)/shard_map/ppermute | solution.py:401
  28.8 7.6 %collective-permute-start.10 = (bf16[392,128]{1,0:T(8,128)(2,1)S(1)}, bf16[392,128]{1,0:T(8,128)(2,1)S(1)}, u32[]{:S(2)}, u32[]{:S(2)}) collective-permute-start(bf16[392,128]{1,0:T(8,128)(2,1)S(1)} %collective-permute-done.3.rest_4_), channel_id=1, source_target_pairs={{0,12},{4,8},{8,4},{12,0},{16,28},{20,24},{24,20},{28,16},{1,13},{... | collective-permute-start | bytes 301064 | tf_op jit(solution)/shard_map/ppermute | solution.py:401
  28.8 7.6 %collective-permute-start.8 = (bf16[392,128]{1,0:T(8,128)(2,1)S(1)}, bf16[392,128]{1,0:T(8,128)(2,1)S(1)}, u32[]{:S(2)}, u32[]{:S(2)}) collective-permute-start(bf16[392,128]{1,0:T(8,128)(2,1)S(1)} %collective-permute-done.3.rest_4_), channel_id=1, source_target_pairs={{0,4},{4,0},{8,12},{12,8},{16,20},{20,16},{24,28},{28,24},{1,5},{5... | collective-permute-start | bytes 301064 | tf_op jit(solution)/shard_map/ppermute | solution.py:401
  30.4 7.1 %collective-permute-start.9 = (bf16[392,128]{1,0:T(8,128)(2,1)S(1)}, bf16[392,128]{1,0:T(8,128)(2,1)S(1)}, u32[]{:S(2)}, u32[]{:S(2)}) collective-permute-start(bf16[392,128]{1,0:T(8,128)(2,1)S(1)} %collective-permute-done.3.rest_4_), channel_id=1, source_target_pairs={{0,8},{4,12},{8,0},{12,4},{16,24},{20,28},{24,16},{28,20},{1,9},{5... | collective-permute-start | bytes 301064 | tf_op jit(solution)/shard_map/ppermute | solution.py:401
  32.3 5.2 %copy-start = (bf16[256,512]{1,0:T(8,128)(2,1)S(1)}, bf16[256,512]{1,0:T(8,128)(2,1)}, u32[]{:S(2)}) copy-start(bf16[256,512]{1,0:T(8,128)(2,1)} %constant.2.clone.table_ref) | copy-start | bytes 786436
  40.8 1.9 %collective-permute-start.11 = (bf16[64,1024]{1,0:T(8,128)(2,1)S(1)}, bf16[64,1024]{1,0:T(8,128)(2,1)S(1)}, u32[]{:S(2)}, u32[]{:S(2)}) collective-permute-start(bf16[64,1024]{1,0:T(8,128)(2,1)S(1)} %get-tuple-element.32), channel_id=1, source_target_pairs={{0,1},{1,0},{2,3},{3,2},{4,5},{5,4},{6,7},{7,6},{8,9},{9,8},{10,11... | collective-permute-start | bytes 393224 | tf_op jit(solution)/shard_map/ppermute | solution.py:401
  40.9 6.4 %collective-permute-start.12 = (bf16[64,1024]{1,0:T(8,128)(2,1)S(1)}, bf16[64,1024]{1,0:T(8,128)(2,1)S(1)}, u32[]{:S(2)}, u32[]{:S(2)}) collective-permute-start(bf16[64,1024]{1,0:T(8,128)(2,1)S(1)} %get-tuple-element.33), channel_id=1, source_target_pairs={{0,2},{1,3},{2,0},{3,1},{4,6},{5,7},{6,4},{7,5},{8,10},{9,11},{10,... | collective-permute-start | bytes 393224 | tf_op jit(solution)/shard_map/ppermute | solution.py:401
  42.5 6.6 %collective-permute-start.13 = (bf16[64,1024]{1,0:T(8,128)(2,1)S(1)}, bf16[64,1024]{1,0:T(8,128)(2,1)S(1)}, u32[]{:S(2)}, u32[]{:S(2)}) collective-permute-start(bf16[64,1024]{1,0:T(8,128)(2,1)S(1)} %get-tuple-element.34), channel_id=1, source_target_pairs={{0,3},{1,2},{2,1},{3,0},{4,7},{5,6},{6,5},{7,4},{8,11},{9,10},{10,... | collective-permute-start | bytes 393224 | tf_op jit(solution)/shard_map/ppermute | solution.py:401

commit v2 on v1

--- a/solution.py
+++ b/solution.py
@@ -313,6 +313,7 @@
 
 
 PER_CHUNK = 8
+IMAGE_PARTS = 2
 
 
 def spectrum_kernel(sizes, direct, *rest):
@@ -340,7 +341,7 @@
         turn_ref[rows, cells:] = cu * sin_v + su * cos_v
 
 
-def image_kernel(sizes, direct, groups, table_ref, early_ref, turn_ref, *rest):
+def image_kernel(sizes, direct, groups, chunks, table_ref, early_ref, turn_ref, *rest):
     count = len(sizes)
     in_refs, out_refs = rest[:count], rest[count : count + groups]
     phases_buf, patch_buf, table_buf = rest[count + groups :]
@@ -353,7 +354,7 @@
     phases = cell_phases(in_refs, sizes, direct)
 
     width = PER_CHUNK * NBLK
-    for chunk in range(NBLK // PER_CHUNK):
+    for i, chunk in enumerate(chunks):
         buf = phases_buf.at[chunk % 2]
         fill_phases(buf, range(chunk * PER_CHUNK, (chunk + 1) * PER_CHUNK), phases)
         here = slice(chunk * width, (chunk + 1) * width)
@@ -365,16 +366,18 @@
             table_buf[...], turned, (((1,), (1,)), ((), ())), preferred_element_type=jnp.float32
         ).astype(jnp.bfloat16)
         for s in range(groups):
-            out_refs[s][:, here] = image[s * share : (s + 1) * share]
-
-
-def finish_kernel(groups, *refs):
-    in_refs, out_ref = refs[:groups], refs[groups]
+            out_refs[s][:, i * width : (i + 1) * width] = image[s * share : (s + 1) * share]
+
+
+def finish_kernel(groups, parts, *refs):
+    out_ref = refs[-1]
     columns = PSIDE // groups
     per_tile = LANES // NBLK
     lane = lax.broadcasted_iota(jnp.int32, (PSIDE, LANES), 1) // NBLK
     for tile in range(NBLK // per_tile):
-        lanes = slice(tile * LANES, (tile + 1) * LANES)
+        part, place = divmod(tile, NBLK // per_tile // parts)
+        in_refs = refs[part * groups : (part + 1) * groups]
+        lanes = slice(place * LANES, (place + 1) * LANES)
         total = in_refs[0][:, lanes].astype(jnp.float32)
         for ref in in_refs[1:]:
             total = total + ref[:, lanes].astype(jnp.float32)
@@ -470,22 +473,26 @@
         name="spectrum",
     )(*early)
     buffers, cost = buffers_and_cost(padded(late_sizes))
-    image = jax.ShapeDtypeStruct((share, points), jnp.bfloat16)
-    images = pl.pallas_call(
-        functools.partial(image_kernel, late_sizes, near, groups),
-        out_shape=[image] * groups,
-        in_specs=[VMEM] * (3 + len(late)),
-        out_specs=[VMEM] * groups,
-        scratch_shapes=buffers + [pltpu.VMEM((cells, 2 * cells), jnp.bfloat16)],
-        compiler_params=compiler_params(40),
-        cost_estimate=cost,
-        name="image",
-    )(jnp.asarray(patch_table(), jnp.bfloat16), spectrum, turns, *late)
-    summed = [images[0]] + [swap(images[s], "freq", s) for s in range(1, groups)]
+    parts = IMAGE_PARTS
+    chunks = NBLK // PER_CHUNK // parts
+    image = jax.ShapeDtypeStruct((share, points // parts), jnp.bfloat16)
+    table = jnp.asarray(patch_table(), jnp.bfloat16)
+    summed = []
+    for part in range(parts):
+        images = pl.pallas_call(
+            functools.partial(image_kernel, late_sizes, near, groups, range(part * chunks, (part + 1) * chunks)),
+            out_shape=[image] * groups,
+            in_specs=[VMEM] * (3 + len(late)),
+            out_specs=[VMEM] * groups,
+            scratch_shapes=buffers + [pltpu.VMEM((cells, 2 * cells), jnp.bfloat16)],
+            compiler_params=compiler_params(40),
+            cost_estimate=cost,
+        )(table, spectrum, turns, *late)
+        summed += [images[0]] + [swap(images[s], "freq", s) for s in range(1, groups)]
     facet_image = pl.pallas_call(
-        functools.partial(finish_kernel, groups),
+        functools.partial(finish_kernel, groups, parts),
         out_shape=jax.ShapeDtypeStruct((GRID, GRID // groups), jnp.float32),
-        in_specs=[VMEM] * groups,
+        in_specs=[VMEM] * len(summed),
         out_specs=VMEM,
         compiler_params=compiler_params(16),
         name="finish",

time: 50.3 us -> 50.3 us (level)
  waiting for transfers between devices: 17.1 us -> 15.1 us
  starting transfers between devices: 20.1 us -> 22 us
    ppermute x14 -> x17, waiting for transfers between devices: 17.1 us -> 15.1 us  [swap(): return lax.ppermute(piece, axis, [(i, i ^ distance) for i in range(count)])]
    ppermute x14 -> x17, starting transfers between devices: 20.1 us -> 22 us  [swap(): return lax.ppermute(piece, axis, [(i, i ^ distance) for i in range(count)])]
    pallas_call x2 -> x3, Pallas kernels: 4.39 us -> 4.46 us  [the longest x2 3.39 us: packed_shards(): pl.pallas_call(functools.partial(image_kernel, late_sizes, near, groups,...]
  transfers between devices with their start and end apart: 14 -> 17, of which waited for: 7 -> 8; matrix products, arithmetic and copies ran while one was open for 0% -> 0% of each run, Pallas kernels for 5% -> 8%
where the time goes in v2:
time: 50.3 us; the launch traced here: 50.2 us
  starting transfers between devices  22 us (44%)
  waiting for transfers between devices  15.1 us (30%)
  Pallas kernels  12.9 us (26%)
    ppermute x17, starting transfers between devices, swap(): return lax.ppermute(piece, axis, [(i, i ^ distance) for i in range(count)])  22 us
    ppermute x17, waiting for transfers between devices, swap(): return lax.ppermute(piece, axis, [(i, i ^ distance) for i in range(count)])  15.1 us
    pallas_call x1, Pallas kernels, packed_shards(): pl.pallas_call(functools.partial(gather_kernel, peers, sizes), out_shape=...  6.06 us
    pallas_call x2, Pallas kernels, packed_shards(): pl.pallas_call(functools.partial(image_kernel, late_sizes, near, groups,...  3.39 us
    pallas_call x1, Pallas kernels, packed_shards(): pl.pallas_call(functools.partial(spectrum_kernel, early_sizes, near), out...  2.43 us
    pallas_call x1, Pallas kernels, packed_shards(): pl.pallas_call(functools.partial(finish_kernel, groups, parts), out_shape...  1.06 us
  transfers between devices with their start and end apart: 17, of which 8 were waited for; matrix products, arithmetic and copies ran while one was open for 0% of the time, Pallas kernels for 8%

profile of v2, /device:TPU:0, one launch (start us, length us, event | category | flops | bytes accessed | tf_op | source)
XLA Modules:
  0.0 50.2 jit_solution(5464409964031314892)
XLA Ops:
  0.0 6.1 %gather.1 = (bf16[520,128]{1,0:T(8,128)(2,1)S(1)}, bf16[520,128]{1,0:T(8,128)(2,1)S(1)}, bf16[520,128]{1,0:T(8,128)(2,1)S(1)}, bf16[520,128]{1,0:T(8,128)(2,1)S(...) custom-call(f32[2,8]{1,0:T(2,128)} %bitcast.13, ...), custom_call_target="tpu_custom_call" | custom-call | tf_op jit(solution)/shard_map/gather/pallas_call | solution.py:435
  6.1 4.1 %collective-permute-start.4 = (bf16[328,128]{1,0:T(8,128)(2,1)S(1)}, bf16[328,128]{1,0:T(8,128)(2,1)S(1)}, u32[]{:S(2)}, u32[]{:S(2)}) collective-permute-start(bf16[328,128]{1,0:T(8,128)(2,1)S(1)} %get-tuple-element.31), channel_id=1, source_target_pairs={{0,16},{4,20},{8,24},{12,28},{16,0},{20,4},{24,8},{28,12},{1,17},{... | collective-permute-start | bytes 251912 | tf_op jit(solution)/shard_map/ppermute | solution.py:404
  10.2 1.5 %collective-permute-start = (bf16[520,128]{1,0:T(8,128)(2,1)S(1)}, bf16[520,128]{1,0:T(8,128)(2,1)S(1)}, u32[]{:S(2)}, u32[]{:S(2)}) collective-permute-start(bf16[520,128]{1,0:T(8,128)(2,1)S(1)} %get-tuple-element.25), channel_id=1, source_target_pairs={{0,4},{4,0},{8,12},{12,8},{16,20},{20,16},{24,28},{28,24},{1,5},{5... | collective-permute-start | bytes 399368 | tf_op jit(solution)/shard_map/ppermute | solution.py:404
  11.7 1.6 %collective-permute-start.1 = (bf16[520,128]{1,0:T(8,128)(2,1)S(1)}, bf16[520,128]{1,0:T(8,128)(2,1)S(1)}, u32[]{:S(2)}, u32[]{:S(2)}) collective-permute-start(bf16[520,128]{1,0:T(8,128)(2,1)S(1)} %get-tuple-element.26), channel_id=1, source_target_pairs={{0,8},{4,12},{8,0},{12,4},{16,24},{20,28},{24,16},{28,20},{1,9},{5... | collective-permute-start | bytes 399368 | tf_op jit(solution)/shard_map/ppermute | solution.py:404
  13.3 0.4 collective-permute-start.2
  13.7 0.1 collective-permute-start.3
  13.8 0.6 %collective-permute-done.4.rest_0_ = bf16[328,128]{1,0:T(8,128)(2,1)S(1)} collective-permute-done((bf16[328,128]{1,0:T(8,128)(2,1)S(1)}, bf16[328,128]{1,0:T(8,128)(2,1)S(1)}, u32[]{:S(2)}, u32[]{:S(2)}) %collective-permute-start.4) | collective-permute-done | bytes 84000 | tf_op jit(solution)/shard_map/ppermute | solution.py:404
  14.4 3.2 %collective-permute-start.5 = (bf16[328,128]{1,0:T(8,128)(2,1)S(1)}, bf16[328,128]{1,0:T(8,128)(2,1)S(1)}, u32[]{:S(2)}, u32[]{:S(2)}) collective-permute-start(bf16[328,128]{1,0:T(8,128)(2,1)S(1)} %get-tuple-element.32), channel_id=1, source_target_pairs={{0,20},{4,16},{8,28},{12,24},{16,4},{20,0},{24,12},{28,8},{1,21},{... | collective-permute-start | bytes 251912 | tf_op jit(solution)/shard_map/ppermute | solution.py:404
  17.6 7.5 %collective-permute-done.5.rest_1_ = bf16[328,128]{1,0:T(8,128)(2,1)S(1)} collective-permute-done((bf16[328,128]{1,0:T(8,128)(2,1)S(1)}, bf16[328,128]{1,0:T(8,128)(2,1)S(1)}, u32[]{:S(2)}, u32[]{:S(2)}) %collective-permute-start.5) | collective-permute-done | bytes 84000 | tf_op jit(solution)/shard_map/ppermute | solution.py:404
  25.0 2.9 %collective-permute-start.6 = (bf16[328,128]{1,0:T(8,128)(2,1)S(1)}, bf16[328,128]{1,0:T(8,128)(2,1)S(1)}, u32[]{:S(2)}, u32[]{:S(2)}) collective-permute-start(bf16[328,128]{1,0:T(8,128)(2,1)S(1)} %get-tuple-element.33), channel_id=1, source_target_pairs={{0,24},{4,28},{8,16},{12,20},{16,8},{20,12},{24,0},{28,4},{1,25},{... | collective-permute-start | bytes 251912 | tf_op jit(solution)/shard_map/ppermute | solution.py:404
  27.9 0.0 collective-permute-done.3.rest_4_
  27.9 0.9 %collective-permute-start.7 = (bf16[328,128]{1,0:T(8,128)(2,1)S(1)}, bf16[328,128]{1,0:T(8,128)(2,1)S(1)}, u32[]{:S(2)}, u32[]{:S(2)}) collective-permute-start(bf16[328,128]{1,0:T(8,128)(2,1)S(1)} %get-tuple-element.34), channel_id=1, source_target_pairs={{0,28},{4,24},{8,20},{12,16},{16,12},{20,8},{24,4},{28,0},{1,29},{... | collective-permute-start | bytes 251912 | tf_op jit(solution)/shard_map/ppermute | solution.py:404
  28.8 0.0 collective-permute-done.rest_1_
  28.8 1.6 %collective-permute-start.8 = (bf16[392,128]{1,0:T(8,128)(2,1)S(1)}, bf16[392,128]{1,0:T(8,128)(2,1)S(1)}, u32[]{:S(2)}, u32[]{:S(2)}) collective-permute-start(bf16[392,128]{1,0:T(8,128)(2,1)S(1)} %collective-permute-done.3.rest_4_), channel_id=1, source_target_pairs={{0,4},{4,0},{8,12},{12,8},{16,20},{20,16},{24,28},{28,24},{1,5},{5... | collective-permute-start | bytes 301064 | tf_op jit(solution)/shard_map/ppermute | solution.py:404
  30.4 1.9 %collective-permute-start.9 = (bf16[392,128]{1,0:T(8,128)(2,1)S(1)}, bf16[392,128]{1,0:T(8,128)(2,1)S(1)}, u32[]{:S(2)}, u32[]{:S(2)}) collective-permute-start(bf16[392,128]{1,0:T(8,128)(2,1)S(1)} %collective-permute-done.3.rest_4_), channel_id=1, source_target_pairs={{0,8},{4,12},{8,0},{12,4},{16,24},{20,28},{24,16},{28,20},{1,9},{5... | collective-permute-start | bytes 301064 | tf_op jit(solution)/shard_map/ppermute | solution.py:404
  32.3 2.4 %spectrum.1 = (f32[1024,512]{1,0:T(8,128)S(1)}, f32[1024,512]{1,0:T(8,128)S(1)}) custom-call(bf16[520,128]{1,0:T(8,128)(2,1)S(1)} %get-tuple-element.24.rest_0_, bf16[520,128]{1,0:T(8,128)(2,1)S(1)} %collective-permute-done.rest_1_, bf16[520,128]{1,0:T(8,128)(2,1)S(1)} %collective-permute-done.1.rest_2_, ...), custom_call_target="tpu_custom_call" | custom-call | flops 1342177280 | bytes 4194304 | tf_op jit(solution)/shard_map/spectrum/pallas_call | solution.py:465
  34.8 0.7 %collective-permute-done.7.rest_3_ = bf16[328,128]{1,0:T(8,128)(2,1)S(1)} collective-permute-done((bf16[328,128]{1,0:T(8,128)(2,1)S(1)}, bf16[328,128]{1,0:T(8,128)(2,1)S(1)}, u32[]{:S(2)}, u32[]{:S(2)}) %collective-permute-start.7) | collective-permute-done | bytes 84000 | tf_op jit(solution)/shard_map/ppermute | solution.py:404
  35.4 1.0 %collective-permute-done.10.rest_6_ = bf16[392,128]{1,0:T(8,128)(2,1)S(1)} collective-permute-done((bf16[392,128]{1,0:T(8,128)(2,1)S(1)}, bf16[392,128]{1,0:T(8,128)(2,1)S(1)}, u32[]{:S(2)}, u32[]{:S(2)}) %collective-permute-start.10) | collective-permute-done | bytes 100384 | tf_op jit(solution)/shard_map/ppermute | solution.py:404
  36.4 0.0 collective-permute-done.8.rest_4_
  36.4 1.1 %collective-permute-done.9.rest_5_ = bf16[392,128]{1,0:T(8,128)(2,1)S(1)} collective-permute-done((bf16[392,128]{1,0:T(8,128)(2,1)S(1)}, bf16[392,128]{1,0:T(8,128)(2,1)S(1)}, u32[]{:S(2)}, u32[]{:S(2)}) %collective-permute-start.9) | collective-permute-done | bytes 100384 | tf_op jit(solution)/shard_map/ppermute | solution.py:404
  37.5 1.7 %shard_map.83 = (bf16[64,512]{1,0:T(8,128)(2,1)S(1)}, bf16[64,512]{1,0:T(8,128)(2,1)S(1)}, bf16[64,512]{1,0:T(8,128)(2,1)S(1)}, bf16[64,512]{1,0:T(8,128)(2,1)S(1)}) custom-call(bf16[256,512]{1,0:T(8,128)(2,1)S(1)} %copy-done, f32[1024,512]{1,0:T(8,128)S(1)} %get-tuple-element.29.early_ref, f32[1024,512]{1,0:T(8,128)S(1)} %get-tuple-element.30.turn_ref, ...), custom_call_target="tpu_custom_call" | custom-call | flops 1342177280 | bytes 4194304 | tf_op jit(solution)/shard_map/pallas_call | solution.py:482
  39.2 0.1 collective-permute-start.14
  39.3 1.5 %collective-permute-start.15 = (bf16[64,512]{1,0:T(8,128)(2,1)S(1)}, bf16[64,512]{1,0:T(8,128)(2,1)S(1)}, u32[]{:S(2)}, u32[]{:S(2)}) collective-permute-start(bf16[64,512]{1,0:T(8,128)(2,1)S(1)} %get-tuple-element.41), channel_id=1, source_target_pairs={{0,2},{1,3},{2,0},{3,1},{4,6},{5,7},{6,4},{7,5},{8,10},{9,11},{10,... | collective-permute-start | bytes 196616 | tf_op jit(solution)/shard_map/ppermute | solution.py:404
  40.8 0.3 collective-permute-start.16
  41.1 1.7 %shard_map.82 = (bf16[64,512]{1,0:T(8,128)(2,1)S(1)}, bf16[64,512]{1,0:T(8,128)(2,1)S(1)}, bf16[64,512]{1,0:T(8,128)(2,1)S(1)}, bf16[64,512]{1,0:T(8,128)(2,1)S(1)}) custom-call(bf16[256,512]{1,0:T(8,128)(2,1)S(1)} %copy-done, f32[1024,512]{1,0:T(8,128)S(1)} %get-tuple-element.29.early_ref, f32[1024,512]{1,0:T(8,128)S(1)} %get-tuple-element.30.turn_ref, ...), custom_call_target="tpu_custom_call" | custom-call | flops 1342177280 | bytes 4194304 | tf_op jit(solution)/shard_map/pallas_call | solution.py:482
  42.8 0.4 collective-permute-start.11
  43.3 1.5 %collective-permute-start.12 = (bf16[64,512]{1,0:T(8,128)(2,1)S(1)}, bf16[64,512]{1,0:T(8,128)(2,1)S(1)}, u32[]{:S(2)}, u32[]{:S(2)}) collective-permute-start(bf16[64,512]{1,0:T(8,128)(2,1)S(1)} %get-tuple-element.37), channel_id=1, source_target_pairs={{0,2},{1,3},{2,0},{3,1},{4,6},{5,7},{6,4},{7,5},{8,10},{9,11},{10,... | collective-permute-start | bytes 196616 | tf_op jit(solution)/shard_map/ppermute | solution.py:404
  44.8 0.0 collective-permute-start.13
  44.8 0.1 collective-permute-done.16.refs_7_
  44.9 2.6 %collective-permute-done.12.refs_2_ = bf16[64,512]{1,0:T(8,128)(2,1)S(1)} collective-permute-done((bf16[64,512]{1,0:T(8,128)(2,1)S(1)}, bf16[64,512]{1,0:T(8,128)(2,1)S(1)}, u32[]{:S(2)}, u32[]{:S(2)}) %collective-permute-start.12) | collective-permute-done | bytes 65568 | tf_op jit(solution)/shard_map/ppermute | solution.py:404
  47.5 1.6 %collective-permute-done.13.refs_3_ = bf16[64,512]{1,0:T(8,128)(2,1)S(1)} collective-permute-done((bf16[64,512]{1,0:T(8,128)(2,1)S(1)}, bf16[64,512]{1,0:T(8,128)(2,1)S(1)}, u32[]{:S(2)}, u32[]{:S(2)}) %collective-permute-start.13) | collective-permute-done | bytes 65568 | tf_op jit(solution)/shard_map/ppermute | solution.py:404
  49.1 1.1 %finish.1 = f32[512,128]{1,0:T(8,128)} custom-call(bf16[64,512]{1,0:T(8,128)(2,1)S(1)} %get-tuple-element.35.refs_0_, bf16[64,512]{1,0:T(8,128)(2,1)S(1)} %collective-permute-done.11.refs_1_, bf16[64,512]{1,0:T(8,128)(2,1)S(1)} %collective-permute-done.12.refs_2_, bf16[64,512]{1,0:T(8,128)(2,1)S(1)} %collective-permute-done.13.refs_3_, ...), custom_call_target="tpu_custom_call" | custom-call | tf_op jit(solution)/shard_map/finish/pallas_call | solution.py:492
  (9 shorter events, 0.0 us)
Async XLA Ops:
  6.1 8.3 %collective-permute-start.4 = (bf16[328,128]{1,0:T(8,128)(2,1)S(1)}, bf16[328,128]{1,0:T(8,128)(2,1)S(1)}, u32[]{:S(2)}, u32[]{:S(2)}) collective-permute-start(bf16[328,128]{1,0:T(8,128)(2,1)S(1)} %get-tuple-element.31), channel_id=1, source_target_pairs={{0,16},{4,20},{8,24},{12,28},{16,0},{20,4},{24,8},{28,12},{1,17},{... | collective-permute-start | bytes 251912 | tf_op jit(solution)/shard_map/ppermute | solution.py:404
  10.2 18.6 %collective-permute-start = (bf16[520,128]{1,0:T(8,128)(2,1)S(1)}, bf16[520,128]{1,0:T(8,128)(2,1)S(1)}, u32[]{:S(2)}, u32[]{:S(2)}) collective-permute-start(bf16[520,128]{1,0:T(8,128)(2,1)S(1)} %get-tuple-element.25), channel_id=1, source_target_pairs={{0,4},{4,0},{8,12},{12,8},{16,20},{20,16},{24,28},{28,24},{1,5},{5... | collective-permute-start | bytes 399368 | tf_op jit(solution)/shard_map/ppermute | solution.py:404
  11.7 17.1 %collective-permute-start.1 = (bf16[520,128]{1,0:T(8,128)(2,1)S(1)}, bf16[520,128]{1,0:T(8,128)(2,1)S(1)}, u32[]{:S(2)}, u32[]{:S(2)}) collective-permute-start(bf16[520,128]{1,0:T(8,128)(2,1)S(1)} %get-tuple-element.26), channel_id=1, source_target_pairs={{0,8},{4,12},{8,0},{12,4},{16,24},{20,28},{24,16},{28,20},{1,9},{5... | collective-permute-start | bytes 399368 | tf_op jit(solution)/shard_map/ppermute | solution.py:404
  13.3 17.1 %collective-permute-start.2 = (bf16[520,128]{1,0:T(8,128)(2,1)S(1)}, bf16[520,128]{1,0:T(8,128)(2,1)S(1)}, u32[]{:S(2)}, u32[]{:S(2)}) collective-permute-start(bf16[520,128]{1,0:T(8,128)(2,1)S(1)} %get-tuple-element.27), channel_id=1, source_target_pairs={{0,12},{4,8},{8,4},{12,0},{16,28},{20,24},{24,20},{28,16},{1,13},{... | collective-permute-start | bytes 399368 | tf_op jit(solution)/shard_map/ppermute | solution.py:404
  13.7 14.2 %collective-permute-start.3 = (bf16[392,128]{1,0:T(8,128)(2,1)S(1)}, bf16[392,128]{1,0:T(8,128)(2,1)S(1)}, u32[]{:S(2)}, u32[]{:S(2)}) collective-permute-start(bf16[392,128]{1,0:T(8,128)(2,1)S(1)} %get-tuple-element.28), channel_id=1, source_target_pairs={{0,16},{4,20},{8,24},{12,28},{16,0},{20,4},{24,8},{28,12},{1,17},{... | collective-permute-start | bytes 301064 | tf_op jit(solution)/shard_map/ppermute | solution.py:404
  14.4 10.7 %collective-permute-start.5 = (bf16[328,128]{1,0:T(8,128)(2,1)S(1)}, bf16[328,128]{1,0:T(8,128)(2,1)S(1)}, u32[]{:S(2)}, u32[]{:S(2)}) collective-permute-start(bf16[328,128]{1,0:T(8,128)(2,1)S(1)} %get-tuple-element.32), channel_id=1, source_target_pairs={{0,20},{4,16},{8,28},{12,24},{16,4},{20,0},{24,12},{28,8},{1,21},{... | collective-permute-start | bytes 251912 | tf_op jit(solution)/shard_map/ppermute | solution.py:404
  25.0 9.7 %collective-permute-start.6 = (bf16[328,128]{1,0:T(8,128)(2,1)S(1)}, bf16[328,128]{1,0:T(8,128)(2,1)S(1)}, u32[]{:S(2)}, u32[]{:S(2)}) collective-permute-start(bf16[328,128]{1,0:T(8,128)(2,1)S(1)} %get-tuple-element.33), channel_id=1, source_target_pairs={{0,24},{4,28},{8,16},{12,20},{16,8},{20,12},{24,0},{28,4},{1,25},{... | collective-permute-start | bytes 251912 | tf_op jit(solution)/shard_map/ppermute | solution.py:404
  27.9 7.5 %collective-permute-start.7 = (bf16[328,128]{1,0:T(8,128)(2,1)S(1)}, bf16[328,128]{1,0:T(8,128)(2,1)S(1)}, u32[]{:S(2)}, u32[]{:S(2)}) collective-permute-start(bf16[328,128]{1,0:T(8,128)(2,1)S(1)} %get-tuple-element.34), channel_id=1, source_target_pairs={{0,28},{4,24},{8,20},{12,16},{16,12},{20,8},{24,4},{28,0},{1,29},{... | collective-permute-start | bytes 251912 | tf_op jit(solution)/shard_map/ppermute | solution.py:404
  28.8 7.6 %collective-permute-start.10 = (bf16[392,128]{1,0:T(8,128)(2,1)S(1)}, bf16[392,128]{1,0:T(8,128)(2,1)S(1)}, u32[]{:S(2)}, u32[]{:S(2)}) collective-permute-start(bf16[392,128]{1,0:T(8,128)(2,1)S(1)} %collective-permute-done.3.rest_4_), channel_id=1, source_target_pairs={{0,12},{4,8},{8,4},{12,0},{16,28},{20,24},{24,20},{28,16},{1,13},{... | collective-permute-start | bytes 301064 | tf_op jit(solution)/shard_map/ppermute | solution.py:404
  28.8 7.6 %collective-permute-start.8 = (bf16[392,128]{1,0:T(8,128)(2,1)S(1)}, bf16[392,128]{1,0:T(8,128)(2,1)S(1)}, u32[]{:S(2)}, u32[]{:S(2)}) collective-permute-start(bf16[392,128]{1,0:T(8,128)(2,1)S(1)} %collective-permute-done.3.rest_4_), channel_id=1, source_target_pairs={{0,4},{4,0},{8,12},{12,8},{16,20},{20,16},{24,28},{28,24},{1,5},{5... | collective-permute-start | bytes 301064 | tf_op jit(solution)/shard_map/ppermute | solution.py:404
  30.4 7.1 %collective-permute-start.9 = (bf16[392,128]{1,0:T(8,128)(2,1)S(1)}, bf16[392,128]{1,0:T(8,128)(2,1)S(1)}, u32[]{:S(2)}, u32[]{:S(2)}) collective-permute-start(bf16[392,128]{1,0:T(8,128)(2,1)S(1)} %collective-permute-done.3.rest_4_), channel_id=1, source_target_pairs={{0,8},{4,12},{8,0},{12,4},{16,24},{20,28},{24,16},{28,20},{1,9},{5... | collective-permute-start | bytes 301064 | tf_op jit(solution)/shard_map/ppermute | solution.py:404
  32.3 5.2 %copy-start = (bf16[256,512]{1,0:T(8,128)(2,1)S(1)}, bf16[256,512]{1,0:T(8,128)(2,1)}, u32[]{:S(2)}) copy-start(bf16[256,512]{1,0:T(8,128)(2,1)} %constant.2.clone.table_ref) | copy-start | bytes 786436
  39.2 5.5 %collective-permute-start.14 = (bf16[64,512]{1,0:T(8,128)(2,1)S(1)}, bf16[64,512]{1,0:T(8,128)(2,1)S(1)}, u32[]{:S(2)}, u32[]{:S(2)}) collective-permute-start(bf16[64,512]{1,0:T(8,128)(2,1)S(1)} %get-tuple-element.40), channel_id=1, source_target_pairs={{0,1},{1,0},{2,3},{3,2},{4,5},{5,4},{6,7},{7,6},{8,9},{9,8},{10,11... | collective-permute-start | bytes 196616 | tf_op jit(solution)/shard_map/ppermute | solution.py:404
  39.3 5.5 %collective-permute-start.15 = (bf16[64,512]{1,0:T(8,128)(2,1)S(1)}, bf16[64,512]{1,0:T(8,128)(2,1)S(1)}, u32[]{:S(2)}, u32[]{:S(2)}) collective-permute-start(bf16[64,512]{1,0:T(8,128)(2,1)S(1)} %get-tuple-element.41), channel_id=1, source_target_pairs={{0,2},{1,3},{2,0},{3,1},{4,6},{5,7},{6,4},{7,5},{8,10},{9,11},{10,... | collective-permute-start | bytes 196616 | tf_op jit(solution)/shard_map/ppermute | solution.py:404
  40.8 4.1 %collective-permute-start.16 = (bf16[64,512]{1,0:T(8,128)(2,1)S(1)}, bf16[64,512]{1,0:T(8,128)(2,1)S(1)}, u32[]{:S(2)}, u32[]{:S(2)}) collective-permute-start(bf16[64,512]{1,0:T(8,128)(2,1)S(1)} %get-tuple-element.42), channel_id=1, source_target_pairs={{0,3},{1,2},{2,1},{3,0},{4,7},{5,6},{6,5},{7,4},{8,11},{9,10},{10,... | collective-permute-start | bytes 196616 | tf_op jit(solution)/shard_map/ppermute | solution.py:404
  42.8 2.1 %collective-permute-start.11 = (bf16[64,512]{1,0:T(8,128)(2,1)S(1)}, bf16[64,512]{1,0:T(8,128)(2,1)S(1)}, u32[]{:S(2)}, u32[]{:S(2)}) collective-permute-start(bf16[64,512]{1,0:T(8,128)(2,1)S(1)} %get-tuple-element.36), channel_id=1, source_target_pairs={{0,1},{1,0},{2,3},{3,2},{4,5},{5,4},{6,7},{7,6},{8,9},{9,8},{10,11... | collective-permute-start | bytes 196616 | tf_op jit(solution)/shard_map/ppermute | solution.py:404
  43.3 4.3 %collective-permute-start.12 = (bf16[64,512]{1,0:T(8,128)(2,1)S(1)}, bf16[64,512]{1,0:T(8,128)(2,1)S(1)}, u32[]{:S(2)}, u32[]{:S(2)}) collective-permute-start(bf16[64,512]{1,0:T(8,128)(2,1)S(1)} %get-tuple-element.37), channel_id=1, source_target_pairs={{0,2},{1,3},{2,0},{3,1},{4,6},{5,7},{6,4},{7,5},{8,10},{9,11},{10,... | collective-permute-start | bytes 196616 | tf_op jit(solution)/shard_map/ppermute | solution.py:404
  44.8 4.3 %collective-permute-start.13 = (bf16[64,512]{1,0:T(8,128)(2,1)S(1)}, bf16[64,512]{1,0:T(8,128)(2,1)S(1)}, u32[]{:S(2)}, u32[]{:S(2)}) collective-permute-start(bf16[64,512]{1,0:T(8,128)(2,1)S(1)} %get-tuple-element.38), channel_id=1, source_target_pairs={{0,3},{1,2},{2,1},{3,0},{4,7},{5,6},{6,5},{7,4},{8,11},{9,10},{10,... | collective-permute-start | bytes 196616 | tf_op jit(solution)/shard_map/ppermute | solution.py:404

commit v3 on v2

--- a/solution.py
+++ b/solution.py
@@ -160,22 +160,24 @@
 
 def gather_kernel(peers, sizes, centers_hbm, facet_hbm, plane_hbm, cell_hbm, vis_hbm, uvw_hbm, kern_hbm, *rest):
     out_refs = rest[: len(sizes)]
-    centers_ref, facet_ref, plane_ref, cell_ref, vis_ref, uvw_ref, kern_ref, parts_ref, rows_ref, sems = rest[len(sizes) :]
+    (centers_ref, facet_ref, plane_ref, cell_ref, vis_ref, uvw_ref, kern_ref, parts_ref, rows_ref, placing_ref, sems) = rest[
+        len(sizes) :
+    ]
     planes, _, depth, cells = kern_ref.shape
     tiles = facet_ref.shape[1]
     half = tiles // 2
     groups_of_lanes = depth // LANES
     rows_of = [slice(h * half, (h + 1) * half) for h in range(2)]
     vis_rows = vis_ref.shape[0] // 2
-    transfers = [(centers_hbm, centers_ref), (facet_hbm, facet_ref), (plane_hbm, plane_ref)]
+    transfers = [(centers_hbm, centers_ref), (facet_hbm, facet_ref), (plane_hbm, plane_ref), (cell_hbm, cell_ref)]
     for h in range(2):
         part = slice(h * vis_rows, (h + 1) * vis_rows)
         transfers += [(vis_hbm.at[part], vis_ref.at[part]), (uvw_hbm.at[:, rows_of[h]], uvw_ref.at[:, rows_of[h]])]
-    transfers += [(cell_hbm, cell_ref)] + [(kern_hbm.at[p], kern_ref.at[p]) for p in range(planes)]
+    transfers += [(kern_hbm.at[p], kern_ref.at[p]) for p in range(planes)]
     copies = [pltpu.make_async_copy(source, target, sems.at[i]) for i, (source, target) in enumerate(transfers)]
     for copy in copies:
         copy.start()
-    for copy in copies[:3]:
+    for copy in copies[:4]:
         copy.wait()
     facet = facet_ref[...]
     l_row = jnp.zeros(facet.shape, jnp.float32)
@@ -201,10 +203,23 @@
     passed = jnp.sum(passed, axis=0, keepdims=True).astype(jnp.int32)
     slot = jnp.where((relative < near) | (rank < few), relative * capacity + rank, peers * capacity + passed)
 
+    placing = lax.broadcasted_iota(jnp.int32, (slots, tiles), 0) == slot
+    placing = placing.astype(jnp.float32).astype(jnp.bfloat16)
+    placing_ref[...] = placing
+    cell = cell_ref[...].astype(jnp.float32)
+    block_u = jnp.floor(cell * (1.0 / NBLK))
+    block_v = cell - block_u * NBLK
+    labels = [block_u, block_v, facet.astype(jnp.float32)] + [zero_row] * (SUBLANES - 3)
+    labels = jnp.concatenate(labels, axis=0).astype(jnp.bfloat16)
+    labels = lax.dot_general(labels, placing, (((1,), (1,)), ((), ())), preferred_element_type=jnp.float32)
+    labels = labels.astype(jnp.bfloat16)
+    for i, (ref, size) in enumerate(zip(out_refs, sizes)):
+        ref[2 * cells // LANES * size :, :] = labels[:, i * LANES : (i + 1) * LANES]
+
     patches = []
     for h in range(2):
         tile_rows = rows_of[h]
-        for copy in copies[3:5] if h == 0 else copies[5:]:
+        for copy in copies[4:6] if h == 0 else copies[6:]:
             copy.wait()
         part = slice(h * vis_rows, (h + 1) * vis_rows)
         parts_ref[part] = vis_ref[part].astype(jnp.float32)
@@ -234,21 +249,11 @@
             total = product if total is None else total + product
         patches.append(jnp.concatenate([total[:half], total[half:]], axis=1).astype(jnp.bfloat16))
     patches = jnp.concatenate(patches, axis=0)
-    placing = lax.broadcasted_iota(jnp.int32, (slots, tiles), 0) == slot
-    placing = placing.astype(jnp.float32).astype(jnp.bfloat16)
-    placed = jnp.dot(placing, patches, preferred_element_type=jnp.float32).astype(jnp.bfloat16)
-    cell = cell_ref[...].astype(jnp.float32)
-    block_u = jnp.floor(cell * (1.0 / NBLK))
-    block_v = cell - block_u * NBLK
-    labels = [block_u, block_v, facet.astype(jnp.float32)] + [zero_row] * (SUBLANES - 3)
-    labels = jnp.concatenate(labels, axis=0).astype(jnp.bfloat16)
-    labels = lax.dot_general(labels, placing, (((1,), (1,)), ((), ())), preferred_element_type=jnp.float32)
-    labels = labels.astype(jnp.bfloat16)
+    placed = jnp.dot(placing_ref[...], patches, preferred_element_type=jnp.float32).astype(jnp.bfloat16)
     for i, (ref, size) in enumerate(zip(out_refs, sizes)):
         start = i * LANES
         for j in range(2 * cells // LANES):
             ref[j * size : (j + 1) * size, :] = placed[start : start + size, j * LANES : (j + 1) * LANES]
-        ref[2 * cells // LANES * size :, :] = labels[:, start : start + LANES]
 
 
 def padded(sizes):
@@ -316,18 +321,28 @@
 IMAGE_PARTS = 2
 
 
-def spectrum_kernel(sizes, direct, *rest):
-    count = len(sizes)
-    in_refs, (out_ref, turn_ref, phases_buf, patch_buf) = rest[:count], rest[count:]
+def add_spectrum(in_refs, sizes, direct, out_ref, phases_buf, patch_buf, start_ref=None):
     load_patches(in_refs, sizes, patch_buf)
     phases = cell_phases(in_refs, sizes, direct)
     width = PER_CHUNK * NBLK
     for chunk in range(NBLK // PER_CHUNK):
+        here = slice(chunk * width, (chunk + 1) * width)
         buf = phases_buf.at[chunk % 2]
         fill_phases(buf, range(chunk * PER_CHUNK, (chunk + 1) * PER_CHUNK), phases)
-        out_ref[chunk * width : (chunk + 1) * width, :] = jnp.dot(
-            buf[...], patch_buf[...], preferred_element_type=jnp.float32
-        )
+        product = jnp.dot(buf[...], patch_buf[...], preferred_element_type=jnp.float32)
+        out_ref[here, :] = product if start_ref is None else start_ref[here, :] + product
+
+
+def middle_kernel(sizes, direct, start_ref, *rest):
+    count = len(sizes)
+    out_ref, phases_buf, patch_buf = rest[count:]
+    add_spectrum(rest[:count], sizes, direct, out_ref, phases_buf, patch_buf, start_ref)
+
+
+def spectrum_kernel(sizes, direct, *rest):
+    count = len(sizes)
+    out_ref, turn_ref, phases_buf, patch_buf = rest[count:]
+    add_spectrum(rest[:count], sizes, direct, out_ref, phases_buf, patch_buf)
 
     cells = PSIDE * PSIDE
     lane = lax.broadcasted_iota(jnp.int32, (NBLK, cells), 1)
@@ -441,6 +456,7 @@
         + [
             pltpu.VMEM(vis_rows.shape, jnp.float32),
             pltpu.VMEM((2, tiles, 2 * depth), jnp.bfloat16),
+            pltpu.VMEM((LANES * len(sizes), tiles), jnp.bfloat16),
             pltpu.SemaphoreType.DMA((len(operands) + 1 + planes,)),
         ],
         compiler_params=compiler_params(40),
@@ -449,8 +465,10 @@
     overflow = [swap(pieces[peers], "facet", near)]
     received = [pieces[0]] + [swap(pieces[s], "facet", s) for s in range(1, peers)]
     overflow += [swap(overflow[0], "facet", s) for s in range(1, near)]
-    early, late = received[:near] + overflow[:1], received[near:] + overflow[1:]
-    early_sizes, late_sizes = sizes[:near] + sizes[peers:], sizes[near:peers] + sizes[peers:] * (near - 1)
+    half = near // 2
+    early, early_sizes = received[:near] + overflow[:1], sizes[:near] + sizes[peers:]
+    middle, middle_sizes = received[near:-half] + overflow[1:], sizes[near : peers - half] + sizes[peers:] * (near - 1)
+    late, late_sizes = received[-half:], sizes[peers - half : peers]
     share = cells // groups
     points = NBLK * NBLK
 
@@ -472,6 +490,17 @@
         cost_estimate=cost,
         name="spectrum",
     )(*early)
+    buffers, cost = buffers_and_cost(padded(middle_sizes))
+    spectrum = pl.pallas_call(
+        functools.partial(middle_kernel, middle_sizes, near - half),
+        out_shape=jax.ShapeDtypeStruct((points, 2 * cells), jnp.float32),
+        in_specs=[VMEM] * (1 + len(middle)),
+        out_specs=VMEM,
+        scratch_shapes=buffers,
+        compiler_params=compiler_params(40),
+        cost_estimate=cost,
+        name="middle",
+    )(spectrum, *middle)
     buffers, cost = buffers_and_cost(padded(late_sizes))
     parts = IMAGE_PARTS
     chunks = NBLK // PER_CHUNK // parts
@@ -480,7 +509,7 @@
     summed = []
     for part in range(parts):
         images = pl.pallas_call(
-            functools.partial(image_kernel, late_sizes, near, groups, range(part * chunks, (part + 1) * chunks)),
+            functools.partial(image_kernel, late_sizes, half, groups, range(part * chunks, (part + 1) * chunks)),
             out_shape=[image] * groups,
             in_specs=[VMEM] * (3 + len(late)),
             out_specs=[VMEM] * groups,

time: 50.3 us -> 49.8 us (0.990)
  waiting for transfers between devices: 15.1 us -> 12.6 us
  starting transfers between devices: 22 us -> 23.9 us
    ppermute x17, waiting for transfers between devices: 15.1 us -> 12.6 us  [swap(): return lax.ppermute(piece, axis, [(i, i ^ distance) for i in range(count)])]
    ppermute x17, starting transfers between devices: 22 us -> 23.9 us  [swap(): return lax.ppermute(piece, axis, [(i, i ^ distance) for i in range(count)])]
    pallas_call x2 -> x3, Pallas kernels: 3.39 us -> 3.65 us  [the longest x2 2.16 us: packed_shards(): pl.pallas_call(functools.partial(image_kernel, late_sizes, half, groups,...]
  transfers between devices with their start and end apart: 17 -> 17, of which waited for: 8 -> 6; matrix products, arithmetic and copies ran while one was open for 0% -> 0% of each run, Pallas kernels for 8% -> 10%
where the time goes in v3:
time: 49.8 us; the launch traced here: 49.7 us
  starting transfers between devices  23.9 us (48%)
  Pallas kernels  13.1 us (26%)
  waiting for transfers between devices  12.6 us (25%)
    ppermute x17, starting transfers between devices, swap(): return lax.ppermute(piece, axis, [(i, i ^ distance) for i in range(count)])  23.9 us
    ppermute x17, waiting for transfers between devices, swap(): return lax.ppermute(piece, axis, [(i, i ^ distance) for i in range(count)])  12.6 us
    pallas_call x1, Pallas kernels, packed_shards(): pl.pallas_call(functools.partial(gather_kernel, peers, sizes), out_shape=...  5.99 us
    pallas_call x1, Pallas kernels, packed_shards(): pl.pallas_call(functools.partial(spectrum_kernel, early_sizes, near), out...  2.43 us
    pallas_call x2, Pallas kernels, packed_shards(): pl.pallas_call(functools.partial(image_kernel, late_sizes, half, groups,...  2.16 us
    pallas_call x1, Pallas kernels, packed_shards(): pl.pallas_call(functools.partial(middle_kernel, middle_sizes, near - half...  1.49 us
    pallas_call x1, Pallas kernels, packed_shards(): pl.pallas_call(functools.partial(finish_kernel, groups, parts), out_shape...  1.07 us
  transfers between devices with their start and end apart: 17, of which 6 were waited for; matrix products, arithmetic and copies ran while one was open for 0% of the time, Pallas kernels for 10%

profile of v3, /device:TPU:0, one launch (start us, length us, event | category | flops | bytes accessed | tf_op | source)
XLA Modules:
  0.0 49.7 jit_solution(7471529833251644377)
XLA Ops:
  0.0 6.0 %gather.1 = (bf16[520,128]{1,0:T(8,128)(2,1)S(1)}, bf16[520,128]{1,0:T(8,128)(2,1)S(1)}, bf16[520,128]{1,0:T(8,128)(2,1)S(1)}, bf16[520,128]{1,0:T(8,128)(2,1)S(...) custom-call(f32[2,8]{1,0:T(2,128)} %bitcast.13, ...), custom_call_target="tpu_custom_call" | custom-call | tf_op jit(solution)/shard_map/gather/pallas_call | solution.py:450
  6.0 3.0 %collective-permute-start = (bf16[520,128]{1,0:T(8,128)(2,1)S(1)}, bf16[520,128]{1,0:T(8,128)(2,1)S(1)}, u32[]{:S(2)}, u32[]{:S(2)}) collective-permute-start(bf16[520,128]{1,0:T(8,128)(2,1)S(1)} %get-tuple-element.25), channel_id=1, source_target_pairs={{0,4},{4,0},{8,12},{12,8},{16,20},{20,16},{24,28},{28,24},{1,5},{5... | collective-permute-start | bytes 399368 | tf_op jit(solution)/shard_map/ppermute | solution.py:419
  9.0 1.6 %collective-permute-start.1 = (bf16[520,128]{1,0:T(8,128)(2,1)S(1)}, bf16[520,128]{1,0:T(8,128)(2,1)S(1)}, u32[]{:S(2)}, u32[]{:S(2)}) collective-permute-start(bf16[520,128]{1,0:T(8,128)(2,1)S(1)} %get-tuple-element.26), channel_id=1, source_target_pairs={{0,8},{4,12},{8,0},{12,4},{16,24},{20,28},{24,16},{28,20},{1,9},{5... | collective-permute-start | bytes 399368 | tf_op jit(solution)/shard_map/ppermute | solution.py:419
  10.6 0.0 collective-permute-start.2
  10.6 3.0 %collective-permute-start.3 = (bf16[392,128]{1,0:T(8,128)(2,1)S(1)}, bf16[392,128]{1,0:T(8,128)(2,1)S(1)}, u32[]{:S(2)}, u32[]{:S(2)}) collective-permute-start(bf16[392,128]{1,0:T(8,128)(2,1)S(1)} %get-tuple-element.28), channel_id=1, source_target_pairs={{0,16},{4,20},{8,24},{12,28},{16,0},{20,4},{24,8},{28,12},{1,17},{... | collective-permute-start | bytes 301064 | tf_op jit(solution)/shard_map/ppermute | solution.py:419
  13.6 0.0 collective-permute-start.4
  13.6 5.5 %collective-permute-done.3.rest_4_ = bf16[392,128]{1,0:T(8,128)(2,1)S(1)} collective-permute-done((bf16[392,128]{1,0:T(8,128)(2,1)S(1)}, bf16[392,128]{1,0:T(8,128)(2,1)S(1)}, u32[]{:S(2)}, u32[]{:S(2)}) %collective-permute-start.3) | collective-permute-done | bytes 100384 | tf_op jit(solution)/shard_map/ppermute | solution.py:419
  19.1 3.4 %collective-permute-start.5 = (bf16[328,128]{1,0:T(8,128)(2,1)S(1)}, bf16[328,128]{1,0:T(8,128)(2,1)S(1)}, u32[]{:S(2)}, u32[]{:S(2)}) collective-permute-start(bf16[328,128]{1,0:T(8,128)(2,1)S(1)} %get-tuple-element.31), channel_id=1, source_target_pairs={{0,20},{4,16},{8,28},{12,24},{16,4},{20,0},{24,12},{28,8},{1,21},{... | collective-permute-start | bytes 251912 | tf_op jit(solution)/shard_map/ppermute | solution.py:419
  22.5 0.0 collective-permute-done.rest_1_
  22.5 0.5 %collective-permute-start.8 = (bf16[392,128]{1,0:T(8,128)(2,1)S(1)}, bf16[392,128]{1,0:T(8,128)(2,1)S(1)}, u32[]{:S(2)}, u32[]{:S(2)}) collective-permute-start(bf16[392,128]{1,0:T(8,128)(2,1)S(1)} %collective-permute-done.3.rest_4_), channel_id=1, source_target_pairs={{0,12},{4,8},{8,4},{12,0},{16,28},{20,24},{24,20},{28,16},{1,13},{... | collective-permute-start | bytes 301064 | tf_op jit(solution)/shard_map/ppermute | solution.py:419
  23.0 0.0 collective-permute-done.1.rest_2_
  23.0 3.2 %collective-permute-start.7 = (bf16[392,128]{1,0:T(8,128)(2,1)S(1)}, bf16[392,128]{1,0:T(8,128)(2,1)S(1)}, u32[]{:S(2)}, u32[]{:S(2)}) collective-permute-start(bf16[392,128]{1,0:T(8,128)(2,1)S(1)} %collective-permute-done.3.rest_4_), channel_id=1, source_target_pairs={{0,8},{4,12},{8,0},{12,4},{16,24},{20,28},{24,16},{28,20},{1,9},{5... | collective-permute-start | bytes 301064 | tf_op jit(solution)/shard_map/ppermute | solution.py:419
  26.2 1.5 %collective-permute-start.6 = (bf16[392,128]{1,0:T(8,128)(2,1)S(1)}, bf16[392,128]{1,0:T(8,128)(2,1)S(1)}, u32[]{:S(2)}, u32[]{:S(2)}) collective-permute-start(bf16[392,128]{1,0:T(8,128)(2,1)S(1)} %collective-permute-done.3.rest_4_), channel_id=1, source_target_pairs={{0,4},{4,0},{8,12},{12,8},{16,20},{20,16},{24,28},{28,24},{1,5},{5... | collective-permute-start | bytes 301064 | tf_op jit(solution)/shard_map/ppermute | solution.py:419
  27.6 2.4 %spectrum.1 = (f32[1024,512]{1,0:T(8,128)S(1)}, f32[1024,512]{1,0:T(8,128)S(1)}) custom-call(bf16[520,128]{1,0:T(8,128)(2,1)S(1)} %get-tuple-element.24.rest_0_, bf16[520,128]{1,0:T(8,128)(2,1)S(1)} %collective-permute-done.rest_1_, bf16[520,128]{1,0:T(8,128)(2,1)S(1)} %collective-permute-done.1.rest_2_, ...), custom_call_target="tpu_custom_call" | custom-call | flops 1342177280 | bytes 4194304 | tf_op jit(solution)/shard_map/spectrum/pallas_call | solution.py:483
  30.1 1.0 %collective-permute-start.9 = (bf16[328,128]{1,0:T(8,128)(2,1)S(1)}, bf16[328,128]{1,0:T(8,128)(2,1)S(1)}, u32[]{:S(2)}, u32[]{:S(2)}) collective-permute-start(bf16[328,128]{1,0:T(8,128)(2,1)S(1)} %get-tuple-element.33), channel_id=1, source_target_pairs={{0,24},{4,28},{8,16},{12,20},{16,8},{20,12},{24,0},{28,4},{1,25},{... | collective-permute-start | bytes 251912 | tf_op jit(solution)/shard_map/ppermute | solution.py:419
  31.1 2.9 %collective-permute-start.10 = (bf16[328,128]{1,0:T(8,128)(2,1)S(1)}, bf16[328,128]{1,0:T(8,128)(2,1)S(1)}, u32[]{:S(2)}, u32[]{:S(2)}) collective-permute-start(bf16[328,128]{1,0:T(8,128)(2,1)S(1)} %get-tuple-element.34), channel_id=1, source_target_pairs={{0,28},{4,24},{8,20},{12,16},{16,12},{20,8},{24,4},{28,0},{1,29},{... | collective-permute-start | bytes 251912 | tf_op jit(solution)/shard_map/ppermute | solution.py:419
  34.0 0.0 copy-start
  34.0 1.5 %middle.1.early_ref = f32[1024,512]{1,0:T(8,128)S(1)} custom-call(f32[1024,512]{1,0:T(8,128)S(1)} %get-tuple-element.29.start_ref, bf16[328,128]{1,0:T(8,128)(2,1)S(1)} %collective-permute-done.4.rest_0_, bf16[328,128]{1,0:T(8,128)(2,1)S(1)} %collective-permute-done.5.rest_1_, bf16[392,128]{1,0:T(8,128)(2,1)S(1)} %collective-permute-done.6.rest_2_, ...), custom_call_target="tpu_custom_call" | custom-call | flops 1073741824 | bytes 4194304 | tf_op jit(solution)/shard_map/middle/pallas_call | solution.py:494
  35.5 1.0 %collective-permute-done.9.rest_0_ = bf16[328,128]{1,0:T(8,128)(2,1)S(1)} collective-permute-done((bf16[328,128]{1,0:T(8,128)(2,1)S(1)}, bf16[328,128]{1,0:T(8,128)(2,1)S(1)}, u32[]{:S(2)}, u32[]{:S(2)}) %collective-permute-start.9) | collective-permute-done | bytes 84000 | tf_op jit(solution)/shard_map/ppermute | solution.py:419
  36.5 1.7 %collective-permute-done.10.rest_1_ = bf16[328,128]{1,0:T(8,128)(2,1)S(1)} collective-permute-done((bf16[328,128]{1,0:T(8,128)(2,1)S(1)}, bf16[328,128]{1,0:T(8,128)(2,1)S(1)}, u32[]{:S(2)}, u32[]{:S(2)}) %collective-permute-start.10) | collective-permute-done | bytes 84000 | tf_op jit(solution)/shard_map/ppermute | solution.py:419
  38.3 1.1 %shard_map.83 = (bf16[64,512]{1,0:T(8,128)(2,1)S(1)}, bf16[64,512]{1,0:T(8,128)(2,1)S(1)}, bf16[64,512]{1,0:T(8,128)(2,1)S(1)}, bf16[64,512]{1,0:T(8,128)(2,1)S(1)}) custom-call(bf16[256,512]{1,0:T(8,128)(2,1)S(1)} %copy-done, f32[1024,512]{1,0:T(8,128)S(1)} %middle.1.early_ref, f32[1024,512]{1,0:T(8,128)S(1)} %get-tuple-element.32.turn_ref, ...), custom_call_target="tpu_custom_call" | custom-call | flops 536870912 | bytes 4194304 | tf_op jit(solution)/shard_map/pallas_call | solution.py:511
  39.3 0.1 collective-permute-start.14
  39.4 1.6 %collective-permute-start.15 = (bf16[64,512]{1,0:T(8,128)(2,1)S(1)}, bf16[64,512]{1,0:T(8,128)(2,1)S(1)}, u32[]{:S(2)}, u32[]{:S(2)}) collective-permute-start(bf16[64,512]{1,0:T(8,128)(2,1)S(1)} %get-tuple-element.41), channel_id=1, source_target_pairs={{0,2},{1,3},{2,0},{3,1},{4,6},{5,7},{6,4},{7,5},{8,10},{9,11},{10,... | collective-permute-start | bytes 196616 | tf_op jit(solution)/shard_map/ppermute | solution.py:419
  41.0 0.3 collective-permute-start.16
  41.3 1.1 %shard_map.82 = (bf16[64,512]{1,0:T(8,128)(2,1)S(1)}, bf16[64,512]{1,0:T(8,128)(2,1)S(1)}, bf16[64,512]{1,0:T(8,128)(2,1)S(1)}, bf16[64,512]{1,0:T(8,128)(2,1)S(1)}) custom-call(bf16[256,512]{1,0:T(8,128)(2,1)S(1)} %copy-done, f32[1024,512]{1,0:T(8,128)S(1)} %middle.1.early_ref, f32[1024,512]{1,0:T(8,128)S(1)} %get-tuple-element.32.turn_ref, ...), custom_call_target="tpu_custom_call" | custom-call | flops 536870912 | bytes 4194304 | tf_op jit(solution)/shard_map/pallas_call | solution.py:511
  42.4 0.4 collective-permute-start.11
  42.8 1.5 %collective-permute-start.12 = (bf16[64,512]{1,0:T(8,128)(2,1)S(1)}, bf16[64,512]{1,0:T(8,128)(2,1)S(1)}, u32[]{:S(2)}, u32[]{:S(2)}) collective-permute-start(bf16[64,512]{1,0:T(8,128)(2,1)S(1)} %get-tuple-element.37), channel_id=1, source_target_pairs={{0,2},{1,3},{2,0},{3,1},{4,6},{5,7},{6,4},{7,5},{8,10},{9,11},{10,... | collective-permute-start | bytes 196616 | tf_op jit(solution)/shard_map/ppermute | solution.py:419
  44.3 0.0 collective-permute-start.13
  44.3 0.7 %collective-permute-done.16.refs_7_ = bf16[64,512]{1,0:T(8,128)(2,1)S(1)} collective-permute-done((bf16[64,512]{1,0:T(8,128)(2,1)S(1)}, bf16[64,512]{1,0:T(8,128)(2,1)S(1)}, u32[]{:S(2)}, u32[]{:S(2)}) %collective-permute-start.16) | collective-permute-done | bytes 65568 | tf_op jit(solution)/shard_map/ppermute | solution.py:419
  45.0 2.0 %collective-permute-done.12.refs_2_ = bf16[64,512]{1,0:T(8,128)(2,1)S(1)} collective-permute-done((bf16[64,512]{1,0:T(8,128)(2,1)S(1)}, bf16[64,512]{1,0:T(8,128)(2,1)S(1)}, u32[]{:S(2)}, u32[]{:S(2)}) %collective-permute-start.12) | collective-permute-done | bytes 65568 | tf_op jit(solution)/shard_map/ppermute | solution.py:419
  47.0 1.6 %collective-permute-done.13.refs_3_ = bf16[64,512]{1,0:T(8,128)(2,1)S(1)} collective-permute-done((bf16[64,512]{1,0:T(8,128)(2,1)S(1)}, bf16[64,512]{1,0:T(8,128)(2,1)S(1)}, u32[]{:S(2)}, u32[]{:S(2)}) %collective-permute-start.13) | collective-permute-done | bytes 65568 | tf_op jit(solution)/shard_map/ppermute | solution.py:419
  48.6 1.1 %finish.1 = f32[512,128]{1,0:T(8,128)} custom-call(bf16[64,512]{1,0:T(8,128)(2,1)S(1)} %get-tuple-element.35.refs_0_, bf16[64,512]{1,0:T(8,128)(2,1)S(1)} %collective-permute-done.11.refs_1_, bf16[64,512]{1,0:T(8,128)(2,1)S(1)} %collective-permute-done.12.refs_2_, bf16[64,512]{1,0:T(8,128)(2,1)S(1)} %collective-permute-done.13.refs_3_, ...), custom_call_target="tpu_custom_call" | custom-call | tf_op jit(solution)/shard_map/finish/pallas_call | solution.py:521
  (10 shorter events, 0.0 us)
Async XLA Ops:
  6.0 16.5 %collective-permute-start = (bf16[520,128]{1,0:T(8,128)(2,1)S(1)}, bf16[520,128]{1,0:T(8,128)(2,1)S(1)}, u32[]{:S(2)}, u32[]{:S(2)}) collective-permute-start(bf16[520,128]{1,0:T(8,128)(2,1)S(1)} %get-tuple-element.25), channel_id=1, source_target_pairs={{0,4},{4,0},{8,12},{12,8},{16,20},{20,16},{24,28},{28,24},{1,5},{5... | collective-permute-start | bytes 399368 | tf_op jit(solution)/shard_map/ppermute | solution.py:419
  9.0 13.9 %collective-permute-start.1 = (bf16[520,128]{1,0:T(8,128)(2,1)S(1)}, bf16[520,128]{1,0:T(8,128)(2,1)S(1)}, u32[]{:S(2)}, u32[]{:S(2)}) collective-permute-start(bf16[520,128]{1,0:T(8,128)(2,1)S(1)} %get-tuple-element.26), channel_id=1, source_target_pairs={{0,8},{4,12},{8,0},{12,4},{16,24},{20,28},{24,16},{28,20},{1,9},{5... | collective-permute-start | bytes 399368 | tf_op jit(solution)/shard_map/ppermute | solution.py:419
  10.6 15.5 %collective-permute-start.2 = (bf16[520,128]{1,0:T(8,128)(2,1)S(1)}, bf16[520,128]{1,0:T(8,128)(2,1)S(1)}, u32[]{:S(2)}, u32[]{:S(2)}) collective-permute-start(bf16[520,128]{1,0:T(8,128)(2,1)S(1)} %get-tuple-element.27), channel_id=1, source_target_pairs={{0,12},{4,8},{8,4},{12,0},{16,28},{20,24},{24,20},{28,16},{1,13},{... | collective-permute-start | bytes 399368 | tf_op jit(solution)/shard_map/ppermute | solution.py:419
  10.6 8.5 %collective-permute-start.3 = (bf16[392,128]{1,0:T(8,128)(2,1)S(1)}, bf16[392,128]{1,0:T(8,128)(2,1)S(1)}, u32[]{:S(2)}, u32[]{:S(2)}) collective-permute-start(bf16[392,128]{1,0:T(8,128)(2,1)S(1)} %get-tuple-element.28), channel_id=1, source_target_pairs={{0,16},{4,20},{8,24},{12,28},{16,0},{20,4},{24,8},{28,12},{1,17},{... | collective-permute-start | bytes 301064 | tf_op jit(solution)/shard_map/ppermute | solution.py:419
  13.6 16.5 %collective-permute-start.4 = (bf16[328,128]{1,0:T(8,128)(2,1)S(1)}, bf16[328,128]{1,0:T(8,128)(2,1)S(1)}, u32[]{:S(2)}, u32[]{:S(2)}) collective-permute-start(bf16[328,128]{1,0:T(8,128)(2,1)S(1)} %get-tuple-element.30), channel_id=1, source_target_pairs={{0,16},{4,20},{8,24},{12,28},{16,0},{20,4},{24,8},{28,12},{1,17},{... | collective-permute-start | bytes 251912 | tf_op jit(solution)/shard_map/ppermute | solution.py:419
  19.1 12.0 %collective-permute-start.5 = (bf16[328,128]{1,0:T(8,128)(2,1)S(1)}, bf16[328,128]{1,0:T(8,128)(2,1)S(1)}, u32[]{:S(2)}, u32[]{:S(2)}) collective-permute-start(bf16[328,128]{1,0:T(8,128)(2,1)S(1)} %get-tuple-element.31), channel_id=1, source_target_pairs={{0,20},{4,16},{8,28},{12,24},{16,4},{20,0},{24,12},{28,8},{1,21},{... | collective-permute-start | bytes 251912 | tf_op jit(solution)/shard_map/ppermute | solution.py:419
  22.5 11.5 %collective-permute-start.8 = (bf16[392,128]{1,0:T(8,128)(2,1)S(1)}, bf16[392,128]{1,0:T(8,128)(2,1)S(1)}, u32[]{:S(2)}, u32[]{:S(2)}) collective-permute-start(bf16[392,128]{1,0:T(8,128)(2,1)S(1)} %collective-permute-done.3.rest_4_), channel_id=1, source_target_pairs={{0,12},{4,8},{8,4},{12,0},{16,28},{20,24},{24,20},{28,16},{1,13},{... | collective-permute-start | bytes 301064 | tf_op jit(solution)/shard_map/ppermute | solution.py:419
  23.0 11.0 %collective-permute-start.7 = (bf16[392,128]{1,0:T(8,128)(2,1)S(1)}, bf16[392,128]{1,0:T(8,128)(2,1)S(1)}, u32[]{:S(2)}, u32[]{:S(2)}) collective-permute-start(bf16[392,128]{1,0:T(8,128)(2,1)S(1)} %collective-permute-done.3.rest_4_), channel_id=1, source_target_pairs={{0,8},{4,12},{8,0},{12,4},{16,24},{20,28},{24,16},{28,20},{1,9},{5... | collective-permute-start | bytes 301064 | tf_op jit(solution)/shard_map/ppermute | solution.py:419
  26.2 7.8 %collective-permute-start.6 = (bf16[392,128]{1,0:T(8,128)(2,1)S(1)}, bf16[392,128]{1,0:T(8,128)(2,1)S(1)}, u32[]{:S(2)}, u32[]{:S(2)}) collective-permute-start(bf16[392,128]{1,0:T(8,128)(2,1)S(1)} %collective-permute-done.3.rest_4_), channel_id=1, source_target_pairs={{0,4},{4,0},{8,12},{12,8},{16,20},{20,16},{24,28},{28,24},{1,5},{5... | collective-permute-start | bytes 301064 | tf_op jit(solution)/shard_map/ppermute | solution.py:419
  30.1 6.4 %collective-permute-start.9 = (bf16[328,128]{1,0:T(8,128)(2,1)S(1)}, bf16[328,128]{1,0:T(8,128)(2,1)S(1)}, u32[]{:S(2)}, u32[]{:S(2)}) collective-permute-start(bf16[328,128]{1,0:T(8,128)(2,1)S(1)} %get-tuple-element.33), channel_id=1, source_target_pairs={{0,24},{4,28},{8,16},{12,20},{16,8},{20,12},{24,0},{28,4},{1,25},{... | collective-permute-start | bytes 251912 | tf_op jit(solution)/shard_map/ppermute | solution.py:419
  31.1 7.2 %collective-permute-start.10 = (bf16[328,128]{1,0:T(8,128)(2,1)S(1)}, bf16[328,128]{1,0:T(8,128)(2,1)S(1)}, u32[]{:S(2)}, u32[]{:S(2)}) collective-permute-start(bf16[328,128]{1,0:T(8,128)(2,1)S(1)} %get-tuple-element.34), channel_id=1, source_target_pairs={{0,28},{4,24},{8,20},{12,16},{16,12},{20,8},{24,4},{28,0},{1,29},{... | collective-permute-start | bytes 251912 | tf_op jit(solution)/shard_map/ppermute | solution.py:419
  34.0 4.3 %copy-start = (bf16[256,512]{1,0:T(8,128)(2,1)S(1)}, bf16[256,512]{1,0:T(8,128)(2,1)}, u32[]{:S(2)}) copy-start(bf16[256,512]{1,0:T(8,128)(2,1)} %constant.2.clone.table_ref) | copy-start | bytes 786436
  39.3 4.9 %collective-permute-start.14 = (bf16[64,512]{1,0:T(8,128)(2,1)S(1)}, bf16[64,512]{1,0:T(8,128)(2,1)S(1)}, u32[]{:S(2)}, u32[]{:S(2)}) collective-permute-start(bf16[64,512]{1,0:T(8,128)(2,1)S(1)} %get-tuple-element.40), channel_id=1, source_target_pairs={{0,1},{1,0},{2,3},{3,2},{4,5},{5,4},{6,7},{7,6},{8,9},{9,8},{10,11... | collective-permute-start | bytes 196616 | tf_op jit(solution)/shard_map/ppermute | solution.py:419
  39.4 4.9 %collective-permute-start.15 = (bf16[64,512]{1,0:T(8,128)(2,1)S(1)}, bf16[64,512]{1,0:T(8,128)(2,1)S(1)}, u32[]{:S(2)}, u32[]{:S(2)}) collective-permute-start(bf16[64,512]{1,0:T(8,128)(2,1)S(1)} %get-tuple-element.41), channel_id=1, source_target_pairs={{0,2},{1,3},{2,0},{3,1},{4,6},{5,7},{6,4},{7,5},{8,10},{9,11},{10,... | collective-permute-start | bytes 196616 | tf_op jit(solution)/shard_map/ppermute | solution.py:419
  41.0 4.1 %collective-permute-start.16 = (bf16[64,512]{1,0:T(8,128)(2,1)S(1)}, bf16[64,512]{1,0:T(8,128)(2,1)S(1)}, u32[]{:S(2)}, u32[]{:S(2)}) collective-permute-start(bf16[64,512]{1,0:T(8,128)(2,1)S(1)} %get-tuple-element.42), channel_id=1, source_target_pairs={{0,3},{1,2},{2,1},{3,0},{4,7},{5,6},{6,5},{7,4},{8,11},{9,10},{10,... | collective-permute-start | bytes 196616 | tf_op jit(solution)/shard_map/ppermute | solution.py:419
  42.4 2.7 %collective-permute-start.11 = (bf16[64,512]{1,0:T(8,128)(2,1)S(1)}, bf16[64,512]{1,0:T(8,128)(2,1)S(1)}, u32[]{:S(2)}, u32[]{:S(2)}) collective-permute-start(bf16[64,512]{1,0:T(8,128)(2,1)S(1)} %get-tuple-element.36), channel_id=1, source_target_pairs={{0,1},{1,0},{2,3},{3,2},{4,5},{5,4},{6,7},{7,6},{8,9},{9,8},{10,11... | collective-permute-start | bytes 196616 | tf_op jit(solution)/shard_map/ppermute | solution.py:419
  42.8 4.3 %collective-permute-start.12 = (bf16[64,512]{1,0:T(8,128)(2,1)S(1)}, bf16[64,512]{1,0:T(8,128)(2,1)S(1)}, u32[]{:S(2)}, u32[]{:S(2)}) collective-permute-start(bf16[64,512]{1,0:T(8,128)(2,1)S(1)} %get-tuple-element.37), channel_id=1, source_target_pairs={{0,2},{1,3},{2,0},{3,1},{4,6},{5,7},{6,4},{7,5},{8,10},{9,11},{10,... | collective-permute-start | bytes 196616 | tf_op jit(solution)/shard_map/ppermute | solution.py:419
  44.3 4.3 %collective-permute-start.13 = (bf16[64,512]{1,0:T(8,128)(2,1)S(1)}, bf16[64,512]{1,0:T(8,128)(2,1)S(1)}, u32[]{:S(2)}, u32[]{:S(2)}) collective-permute-start(bf16[64,512]{1,0:T(8,128)(2,1)S(1)} %get-tuple-element.38), channel_id=1, source_target_pairs={{0,3},{1,2},{2,1},{3,0},{4,7},{5,6},{6,5},{7,4},{8,11},{9,10},{10,... | collective-permute-start | bytes 196616 | tf_op jit(solution)/shard_map/ppermute | solution.py:419

commit v4 on v3

--- a/solution.py
+++ b/solution.py
@@ -216,10 +216,9 @@
     for i, (ref, size) in enumerate(zip(out_refs, sizes)):
         ref[2 * cells // LANES * size :, :] = labels[:, i * LANES : (i + 1) * LANES]
 
-    patches = []
     for h in range(2):
         tile_rows = rows_of[h]
-        for copy in copies[4:6] if h == 0 else copies[6:]:
+        for copy in copies[4 + 2 * h : 6 + 2 * h]:
             copy.wait()
         part = slice(h * vis_rows, (h + 1) * vis_rows)
         parts_ref[part] = vis_ref[part].astype(jnp.float32)
@@ -238,16 +237,19 @@
             rows_ref[h, :half, right] = -rot_imag
             rows_ref[h, half:, lane] = rot_imag
             rows_ref[h, half:, right] = rot_real
-    for h in range(2):
-        plane_two = jnp.concatenate([columns[rows_of[h], 3:4]] * 2, axis=0)
-        total = None
-        for p in range(planes):
-            mask = (plane_two == float(p)).astype(jnp.float32).astype(jnp.bfloat16)
-            product = jnp.dot(
-                rows_ref[h] * mask, kern_ref[p].reshape(2 * depth, cells), preferred_element_type=jnp.float32
-            )
-            total = product if total is None else total + product
-        patches.append(jnp.concatenate([total[:half], total[half:]], axis=1).astype(jnp.bfloat16))
+    totals = [None, None]
+    for chosen in (range(planes // 2), range(planes // 2, planes)):
+        for p in chosen:
+            copies[8 + p].wait()
+        for h in range(2):
+            plane_two = jnp.concatenate([columns[rows_of[h], 3:4]] * 2, axis=0)
+            for p in chosen:
+                mask = (plane_two == float(p)).astype(jnp.float32).astype(jnp.bfloat16)
+                product = jnp.dot(
+                    rows_ref[h] * mask, kern_ref[p].reshape(2 * depth, cells), preferred_element_type=jnp.float32
+                )
+                totals[h] = product if totals[h] is None else totals[h] + product
+    patches = [jnp.concatenate([total[:half], total[half:]], axis=1).astype(jnp.bfloat16) for total in totals]
     patches = jnp.concatenate(patches, axis=0)
     placed = jnp.dot(placing_ref[...], patches, preferred_element_type=jnp.float32).astype(jnp.bfloat16)
     for i, (ref, size) in enumerate(zip(out_refs, sizes)):
@@ -465,10 +467,9 @@
     overflow = [swap(pieces[peers], "facet", near)]
     received = [pieces[0]] + [swap(pieces[s], "facet", s) for s in range(1, peers)]
     overflow += [swap(overflow[0], "facet", s) for s in range(1, near)]
-    half = near // 2
     early, early_sizes = received[:near] + overflow[:1], sizes[:near] + sizes[peers:]
-    middle, middle_sizes = received[near:-half] + overflow[1:], sizes[near : peers - half] + sizes[peers:] * (near - 1)
-    late, late_sizes = received[-half:], sizes[peers - half : peers]
+    middle, middle_sizes = received[near:-1], sizes[near : peers - 1]
+    late, late_sizes = received[-1:] + overflow[1:], sizes[peers - 1 : peers] + sizes[peers:] * (near - 1)
     share = cells // groups
     points = NBLK * NBLK
 
@@ -492,7 +493,7 @@
     )(*early)
     buffers, cost = buffers_and_cost(padded(middle_sizes))
     spectrum = pl.pallas_call(
-        functools.partial(middle_kernel, middle_sizes, near - half),
+        functools.partial(middle_kernel, middle_sizes, near - 1),
         out_shape=jax.ShapeDtypeStruct((points, 2 * cells), jnp.float32),
         in_specs=[VMEM] * (1 + len(middle)),
         out_specs=VMEM,
@@ -509,7 +510,7 @@
     summed = []
     for part in range(parts):
         images = pl.pallas_call(
-            functools.partial(image_kernel, late_sizes, half, groups, range(part * chunks, (part + 1) * chunks)),
+            functools.partial(image_kernel, late_sizes, 1, groups, range(part * chunks, (part + 1) * chunks)),
             out_shape=[image] * groups,
             in_specs=[VMEM] * (3 + len(late)),
             out_specs=[VMEM] * groups,

time: 49.8 us -> 48.6 us (0.976)
  starting transfers between devices: 23.9 us -> 22 us
  waiting for transfers between devices: 12.6 us -> 14.3 us
  Pallas kernels: 13.1 us -> 12.1 us
    ppermute x17, starting transfers between devices: 23.9 us -> 22 us  [swap(): return lax.ppermute(piece, axis, [(i, i ^ distance) for i in range(count)])]
    ppermute x17, waiting for transfers between devices: 12.6 us -> 14.3 us  [swap(): return lax.ppermute(piece, axis, [(i, i ^ distance) for i in range(count)])]
    pallas_call x1, Pallas kernels: 5.99 us -> 5.2 us  [packed_shards(): pl.pallas_call(functools.partial(gather_kernel, peers, sizes), out_shape=...]
  transfers between devices with their start and end apart: 17 -> 17, of which waited for: 6 -> 7; matrix products, arithmetic and copies ran while one was open for 0% -> 0% of each run, Pallas kernels for 10% -> 9%
where the time goes in v4:
time: 48.6 us; the launch traced here: 48.4 us
  starting transfers between devices  22 us (45%)
  waiting for transfers between devices  14.3 us (29%)
  Pallas kernels  12.1 us (25%)
    ppermute x17, starting transfers between devices, swap(): return lax.ppermute(piece, axis, [(i, i ^ distance) for i in range(count)])  22 us
    ppermute x17, waiting for transfers between devices, swap(): return lax.ppermute(piece, axis, [(i, i ^ distance) for i in range(count)])  14.3 us
    pallas_call x1, Pallas kernels, packed_shards(): pl.pallas_call(functools.partial(gather_kernel, peers, sizes), out_shape=...  5.2 us
    pallas_call x2, Pallas kernels, packed_shards(): pl.pallas_call(functools.partial(image_kernel, late_sizes, 1, groups, ran...  2.52 us
    pallas_call x1, Pallas kernels, packed_shards(): pl.pallas_call(functools.partial(spectrum_kernel, early_sizes, near), out...  2.42 us
    pallas_call x1, Pallas kernels, packed_shards(): pl.pallas_call(functools.partial(finish_kernel, groups, parts), out_shape...  1.06 us
  transfers between devices with their start and end apart: 17, of which 7 were waited for; matrix products, arithmetic and copies ran while one was open for 0% of the time, Pallas kernels for 9%

profile of v4, /device:TPU:0, one launch (start us, length us, event | category | flops | bytes accessed | tf_op | source)
XLA Modules:
  0.0 48.4 jit_solution(288009552393063573)
XLA Ops:
  0.0 5.2 %gather.1 = (bf16[520,128]{1,0:T(8,128)(2,1)S(1)}, bf16[520,128]{1,0:T(8,128)(2,1)S(1)}, bf16[520,128]{1,0:T(8,128)(2,1)S(1)}, bf16[520,128]{1,0:T(8,128)(2,1)S(...) custom-call(f32[2,8]{1,0:T(2,128)} %bitcast.13, ...), custom_call_target="tpu_custom_call" | custom-call | tf_op jit(solution)/shard_map/gather/pallas_call | solution.py:452
  5.2 4.1 %collective-permute-start.4 = (bf16[328,128]{1,0:T(8,128)(2,1)S(1)}, bf16[328,128]{1,0:T(8,128)(2,1)S(1)}, u32[]{:S(2)}, u32[]{:S(2)}) collective-permute-start(bf16[328,128]{1,0:T(8,128)(2,1)S(1)} %get-tuple-element.30), channel_id=1, source_target_pairs={{0,16},{4,20},{8,24},{12,28},{16,0},{20,4},{24,8},{28,12},{1,17},{... | collective-permute-start | bytes 251912 | tf_op jit(solution)/shard_map/ppermute | solution.py:421
  9.3 1.5 %collective-permute-start = (bf16[520,128]{1,0:T(8,128)(2,1)S(1)}, bf16[520,128]{1,0:T(8,128)(2,1)S(1)}, u32[]{:S(2)}, u32[]{:S(2)}) collective-permute-start(bf16[520,128]{1,0:T(8,128)(2,1)S(1)} %get-tuple-element.25), channel_id=1, source_target_pairs={{0,4},{4,0},{8,12},{12,8},{16,20},{20,16},{24,28},{28,24},{1,5},{5... | collective-permute-start | bytes 399368 | tf_op jit(solution)/shard_map/ppermute | solution.py:421
  10.9 1.6 %collective-permute-start.1 = (bf16[520,128]{1,0:T(8,128)(2,1)S(1)}, bf16[520,128]{1,0:T(8,128)(2,1)S(1)}, u32[]{:S(2)}, u32[]{:S(2)}) collective-permute-start(bf16[520,128]{1,0:T(8,128)(2,1)S(1)} %get-tuple-element.26), channel_id=1, source_target_pairs={{0,8},{4,12},{8,0},{12,4},{16,24},{20,28},{24,16},{28,20},{1,9},{5... | collective-permute-start | bytes 399368 | tf_op jit(solution)/shard_map/ppermute | solution.py:421
  12.4 0.4 collective-permute-start.2
  12.8 0.1 collective-permute-start.3
  12.9 0.6 %collective-permute-done.4.rest_0_ = bf16[328,128]{1,0:T(8,128)(2,1)S(1)} collective-permute-done((bf16[328,128]{1,0:T(8,128)(2,1)S(1)}, bf16[328,128]{1,0:T(8,128)(2,1)S(1)}, u32[]{:S(2)}, u32[]{:S(2)}) %collective-permute-start.4) | collective-permute-done | bytes 84000 | tf_op jit(solution)/shard_map/ppermute | solution.py:421
  13.5 3.2 %collective-permute-start.5 = (bf16[328,128]{1,0:T(8,128)(2,1)S(1)}, bf16[328,128]{1,0:T(8,128)(2,1)S(1)}, u32[]{:S(2)}, u32[]{:S(2)}) collective-permute-start(bf16[328,128]{1,0:T(8,128)(2,1)S(1)} %get-tuple-element.31), channel_id=1, source_target_pairs={{0,20},{4,16},{8,28},{12,24},{16,4},{20,0},{24,12},{28,8},{1,21},{... | collective-permute-start | bytes 251912 | tf_op jit(solution)/shard_map/ppermute | solution.py:421
  16.7 7.5 %collective-permute-done.5.rest_1_ = bf16[328,128]{1,0:T(8,128)(2,1)S(1)} collective-permute-done((bf16[328,128]{1,0:T(8,128)(2,1)S(1)}, bf16[328,128]{1,0:T(8,128)(2,1)S(1)}, u32[]{:S(2)}, u32[]{:S(2)}) %collective-permute-start.5) | collective-permute-done | bytes 84000 | tf_op jit(solution)/shard_map/ppermute | solution.py:421
  24.2 2.9 %collective-permute-start.6 = (bf16[328,128]{1,0:T(8,128)(2,1)S(1)}, bf16[328,128]{1,0:T(8,128)(2,1)S(1)}, u32[]{:S(2)}, u32[]{:S(2)}) collective-permute-start(bf16[328,128]{1,0:T(8,128)(2,1)S(1)} %get-tuple-element.32), channel_id=1, source_target_pairs={{0,24},{4,28},{8,16},{12,20},{16,8},{20,12},{24,0},{28,4},{1,25},{... | collective-permute-start | bytes 251912 | tf_op jit(solution)/shard_map/ppermute | solution.py:421
  27.0 0.9 %collective-permute-start.7 = (bf16[328,128]{1,0:T(8,128)(2,1)S(1)}, bf16[328,128]{1,0:T(8,128)(2,1)S(1)}, u32[]{:S(2)}, u32[]{:S(2)}) collective-permute-start(bf16[328,128]{1,0:T(8,128)(2,1)S(1)} %get-tuple-element.34), channel_id=1, source_target_pairs={{0,28},{4,24},{8,20},{12,16},{16,12},{20,8},{24,4},{28,0},{1,29},{... | collective-permute-start | bytes 251912 | tf_op jit(solution)/shard_map/ppermute | solution.py:421
  27.9 0.0 collective-permute-done.rest_1_
  28.0 1.6 %collective-permute-start.8 = (bf16[392,128]{1,0:T(8,128)(2,1)S(1)}, bf16[392,128]{1,0:T(8,128)(2,1)S(1)}, u32[]{:S(2)}, u32[]{:S(2)}) collective-permute-start(bf16[392,128]{1,0:T(8,128)(2,1)S(1)} %collective-permute-done.3.rest_4_), channel_id=1, source_target_pairs={{0,4},{4,0},{8,12},{12,8},{16,20},{20,16},{24,28},{28,24},{1,5},{5... | collective-permute-start | bytes 301064 | tf_op jit(solution)/shard_map/ppermute | solution.py:421
  29.5 1.9 %collective-permute-start.9 = (bf16[392,128]{1,0:T(8,128)(2,1)S(1)}, bf16[392,128]{1,0:T(8,128)(2,1)S(1)}, u32[]{:S(2)}, u32[]{:S(2)}) collective-permute-start(bf16[392,128]{1,0:T(8,128)(2,1)S(1)} %collective-permute-done.3.rest_4_), channel_id=1, source_target_pairs={{0,8},{4,12},{8,0},{12,4},{16,24},{20,28},{24,16},{28,20},{1,9},{5... | collective-permute-start | bytes 301064 | tf_op jit(solution)/shard_map/ppermute | solution.py:421
  31.4 2.4 %spectrum.1 = (f32[1024,512]{1,0:T(8,128)S(1)}, f32[1024,512]{1,0:T(8,128)S(1)}) custom-call(bf16[520,128]{1,0:T(8,128)(2,1)S(1)} %get-tuple-element.24.rest_0_, bf16[520,128]{1,0:T(8,128)(2,1)S(1)} %collective-permute-done.rest_1_, bf16[520,128]{1,0:T(8,128)(2,1)S(1)} %collective-permute-done.1.rest_2_, ...), custom_call_target="tpu_custom_call" | custom-call | flops 1342177280 | bytes 4194304 | tf_op jit(solution)/shard_map/spectrum/pallas_call | solution.py:484
  33.9 0.0 copy-start
  33.9 0.9 %middle.1.early_ref = f32[1024,512]{1,0:T(8,128)S(1)} custom-call(f32[1024,512]{1,0:T(8,128)S(1)} %get-tuple-element.29.start_ref, bf16[328,128]{1,0:T(8,128)(2,1)S(1)} %collective-permute-done.4.rest_0_, bf16[328,128]{1,0:T(8,128)(2,1)S(1)} %collective-permute-done.5.rest_1_, bf16[328,128]{1,0:T(8,128)(2,1)S(1)} %collective-permute-done.6.rest_2_), custom_call_target="tpu_custom_call" | custom-call | flops 536870912 | bytes 4194304 | tf_op jit(solution)/shard_map/middle/pallas_call | solution.py:495
  34.8 0.7 %collective-permute-done.10.rest_3_ = bf16[392,128]{1,0:T(8,128)(2,1)S(1)} collective-permute-done((bf16[392,128]{1,0:T(8,128)(2,1)S(1)}, bf16[392,128]{1,0:T(8,128)(2,1)S(1)}, u32[]{:S(2)}, u32[]{:S(2)}) %collective-permute-start.10) | collective-permute-done | bytes 100384 | tf_op jit(solution)/shard_map/ppermute | solution.py:421
  35.5 0.0 collective-permute-done.8.rest_1_
  35.5 1.1 %collective-permute-done.9.rest_2_ = bf16[392,128]{1,0:T(8,128)(2,1)S(1)} collective-permute-done((bf16[392,128]{1,0:T(8,128)(2,1)S(1)}, bf16[392,128]{1,0:T(8,128)(2,1)S(1)}, u32[]{:S(2)}, u32[]{:S(2)}) %collective-permute-start.9) | collective-permute-done | bytes 100384 | tf_op jit(solution)/shard_map/ppermute | solution.py:421
  36.6 1.3 %shard_map.83 = (bf16[64,512]{1,0:T(8,128)(2,1)S(1)}, bf16[64,512]{1,0:T(8,128)(2,1)S(1)}, bf16[64,512]{1,0:T(8,128)(2,1)S(1)}, bf16[64,512]{1,0:T(8,128)(2,1)S(1)}) custom-call(bf16[256,512]{1,0:T(8,128)(2,1)S(1)} %copy-done, f32[1024,512]{1,0:T(8,128)S(1)} %middle.1.early_ref, f32[1024,512]{1,0:T(8,128)S(1)} %get-tuple-element.33.turn_ref, ...), custom_call_target="tpu_custom_call" | custom-call | flops 805306368 | bytes 4194304 | tf_op jit(solution)/shard_map/pallas_call | solution.py:512
  37.9 0.1 collective-permute-start.14
  38.0 1.6 %collective-permute-start.15 = (bf16[64,512]{1,0:T(8,128)(2,1)S(1)}, bf16[64,512]{1,0:T(8,128)(2,1)S(1)}, u32[]{:S(2)}, u32[]{:S(2)}) collective-permute-start(bf16[64,512]{1,0:T(8,128)(2,1)S(1)} %get-tuple-element.41), channel_id=1, source_target_pairs={{0,2},{1,3},{2,0},{3,1},{4,6},{5,7},{6,4},{7,5},{8,10},{9,11},{10,... | collective-permute-start | bytes 196616 | tf_op jit(solution)/shard_map/ppermute | solution.py:421
  39.5 0.3 collective-permute-start.16
  39.8 1.3 %shard_map.82 = (bf16[64,512]{1,0:T(8,128)(2,1)S(1)}, bf16[64,512]{1,0:T(8,128)(2,1)S(1)}, bf16[64,512]{1,0:T(8,128)(2,1)S(1)}, bf16[64,512]{1,0:T(8,128)(2,1)S(1)}) custom-call(bf16[256,512]{1,0:T(8,128)(2,1)S(1)} %copy-done, f32[1024,512]{1,0:T(8,128)S(1)} %middle.1.early_ref, f32[1024,512]{1,0:T(8,128)S(1)} %get-tuple-element.33.turn_ref, ...), custom_call_target="tpu_custom_call" | custom-call | flops 805306368 | bytes 4194304 | tf_op jit(solution)/shard_map/pallas_call | solution.py:512
  41.1 0.4 collective-permute-start.11
  41.5 1.5 %collective-permute-start.12 = (bf16[64,512]{1,0:T(8,128)(2,1)S(1)}, bf16[64,512]{1,0:T(8,128)(2,1)S(1)}, u32[]{:S(2)}, u32[]{:S(2)}) collective-permute-start(bf16[64,512]{1,0:T(8,128)(2,1)S(1)} %get-tuple-element.37), channel_id=1, source_target_pairs={{0,2},{1,3},{2,0},{3,1},{4,6},{5,7},{6,4},{7,5},{8,10},{9,11},{10,... | collective-permute-start | bytes 196616 | tf_op jit(solution)/shard_map/ppermute | solution.py:421
  43.0 0.0 collective-permute-start.13
  43.0 0.6 %collective-permute-done.16.refs_7_ = bf16[64,512]{1,0:T(8,128)(2,1)S(1)} collective-permute-done((bf16[64,512]{1,0:T(8,128)(2,1)S(1)}, bf16[64,512]{1,0:T(8,128)(2,1)S(1)}, u32[]{:S(2)}, u32[]{:S(2)}) %collective-permute-start.16) | collective-permute-done | bytes 65568 | tf_op jit(solution)/shard_map/ppermute | solution.py:421
  43.6 2.2 %collective-permute-done.12.refs_2_ = bf16[64,512]{1,0:T(8,128)(2,1)S(1)} collective-permute-done((bf16[64,512]{1,0:T(8,128)(2,1)S(1)}, bf16[64,512]{1,0:T(8,128)(2,1)S(1)}, u32[]{:S(2)}, u32[]{:S(2)}) %collective-permute-start.12) | collective-permute-done | bytes 65568 | tf_op jit(solution)/shard_map/ppermute | solution.py:421
  45.8 1.6 %collective-permute-done.13.refs_3_ = bf16[64,512]{1,0:T(8,128)(2,1)S(1)} collective-permute-done((bf16[64,512]{1,0:T(8,128)(2,1)S(1)}, bf16[64,512]{1,0:T(8,128)(2,1)S(1)}, u32[]{:S(2)}, u32[]{:S(2)}) %collective-permute-start.13) | collective-permute-done | bytes 65568 | tf_op jit(solution)/shard_map/ppermute | solution.py:421
  47.4 1.1 %finish.1 = f32[512,128]{1,0:T(8,128)} custom-call(bf16[64,512]{1,0:T(8,128)(2,1)S(1)} %get-tuple-element.35.refs_0_, bf16[64,512]{1,0:T(8,128)(2,1)S(1)} %collective-permute-done.11.refs_1_, bf16[64,512]{1,0:T(8,128)(2,1)S(1)} %collective-permute-done.12.refs_2_, bf16[64,512]{1,0:T(8,128)(2,1)S(1)} %collective-permute-done.13.refs_3_, ...), custom_call_target="tpu_custom_call" | custom-call | tf_op jit(solution)/shard_map/finish/pallas_call | solution.py:522
  (10 shorter events, 0.0 us)
Async XLA Ops:
  5.2 8.3 %collective-permute-start.4 = (bf16[328,128]{1,0:T(8,128)(2,1)S(1)}, bf16[328,128]{1,0:T(8,128)(2,1)S(1)}, u32[]{:S(2)}, u32[]{:S(2)}) collective-permute-start(bf16[328,128]{1,0:T(8,128)(2,1)S(1)} %get-tuple-element.30), channel_id=1, source_target_pairs={{0,16},{4,20},{8,24},{12,28},{16,0},{20,4},{24,8},{28,12},{1,17},{... | collective-permute-start | bytes 251912 | tf_op jit(solution)/shard_map/ppermute | solution.py:421
  9.3 18.6 %collective-permute-start = (bf16[520,128]{1,0:T(8,128)(2,1)S(1)}, bf16[520,128]{1,0:T(8,128)(2,1)S(1)}, u32[]{:S(2)}, u32[]{:S(2)}) collective-permute-start(bf16[520,128]{1,0:T(8,128)(2,1)S(1)} %get-tuple-element.25), channel_id=1, source_target_pairs={{0,4},{4,0},{8,12},{12,8},{16,20},{20,16},{24,28},{28,24},{1,5},{5... | collective-permute-start | bytes 399368 | tf_op jit(solution)/shard_map/ppermute | solution.py:421
  10.9 17.1 %collective-permute-start.1 = (bf16[520,128]{1,0:T(8,128)(2,1)S(1)}, bf16[520,128]{1,0:T(8,128)(2,1)S(1)}, u32[]{:S(2)}, u32[]{:S(2)}) collective-permute-start(bf16[520,128]{1,0:T(8,128)(2,1)S(1)} %get-tuple-element.26), channel_id=1, source_target_pairs={{0,8},{4,12},{8,0},{12,4},{16,24},{20,28},{24,16},{28,20},{1,9},{5... | collective-permute-start | bytes 399368 | tf_op jit(solution)/shard_map/ppermute | solution.py:421
  12.4 17.1 %collective-permute-start.2 = (bf16[520,128]{1,0:T(8,128)(2,1)S(1)}, bf16[520,128]{1,0:T(8,128)(2,1)S(1)}, u32[]{:S(2)}, u32[]{:S(2)}) collective-permute-start(bf16[520,128]{1,0:T(8,128)(2,1)S(1)} %get-tuple-element.27), channel_id=1, source_target_pairs={{0,12},{4,8},{8,4},{12,0},{16,28},{20,24},{24,20},{28,16},{1,13},{... | collective-permute-start | bytes 399368 | tf_op jit(solution)/shard_map/ppermute | solution.py:421
  12.8 14.2 %collective-permute-start.3 = (bf16[392,128]{1,0:T(8,128)(2,1)S(1)}, bf16[392,128]{1,0:T(8,128)(2,1)S(1)}, u32[]{:S(2)}, u32[]{:S(2)}) collective-permute-start(bf16[392,128]{1,0:T(8,128)(2,1)S(1)} %get-tuple-element.28), channel_id=1, source_target_pairs={{0,16},{4,20},{8,24},{12,28},{16,0},{20,4},{24,8},{28,12},{1,17},{... | collective-permute-start | bytes 301064 | tf_op jit(solution)/shard_map/ppermute | solution.py:421
  13.5 10.6 %collective-permute-start.5 = (bf16[328,128]{1,0:T(8,128)(2,1)S(1)}, bf16[328,128]{1,0:T(8,128)(2,1)S(1)}, u32[]{:S(2)}, u32[]{:S(2)}) collective-permute-start(bf16[328,128]{1,0:T(8,128)(2,1)S(1)} %get-tuple-element.31), channel_id=1, source_target_pairs={{0,20},{4,16},{8,28},{12,24},{16,4},{20,0},{24,12},{28,8},{1,21},{... | collective-permute-start | bytes 251912 | tf_op jit(solution)/shard_map/ppermute | solution.py:421
  24.2 9.7 %collective-permute-start.6 = (bf16[328,128]{1,0:T(8,128)(2,1)S(1)}, bf16[328,128]{1,0:T(8,128)(2,1)S(1)}, u32[]{:S(2)}, u32[]{:S(2)}) collective-permute-start(bf16[328,128]{1,0:T(8,128)(2,1)S(1)} %get-tuple-element.32), channel_id=1, source_target_pairs={{0,24},{4,28},{8,16},{12,20},{16,8},{20,12},{24,0},{28,4},{1,25},{... | collective-permute-start | bytes 251912 | tf_op jit(solution)/shard_map/ppermute | solution.py:421
  27.0 7.7 %collective-permute-start.7 = (bf16[328,128]{1,0:T(8,128)(2,1)S(1)}, bf16[328,128]{1,0:T(8,128)(2,1)S(1)}, u32[]{:S(2)}, u32[]{:S(2)}) collective-permute-start(bf16[328,128]{1,0:T(8,128)(2,1)S(1)} %get-tuple-element.34), channel_id=1, source_target_pairs={{0,28},{4,24},{8,20},{12,16},{16,12},{20,8},{24,4},{28,0},{1,29},{... | collective-permute-start | bytes 251912 | tf_op jit(solution)/shard_map/ppermute | solution.py:421
  27.9 7.6 %collective-permute-start.10 = (bf16[392,128]{1,0:T(8,128)(2,1)S(1)}, bf16[392,128]{1,0:T(8,128)(2,1)S(1)}, u32[]{:S(2)}, u32[]{:S(2)}) collective-permute-start(bf16[392,128]{1,0:T(8,128)(2,1)S(1)} %collective-permute-done.3.rest_4_), channel_id=1, source_target_pairs={{0,12},{4,8},{8,4},{12,0},{16,28},{20,24},{24,20},{28,16},{1,13},{... | collective-permute-start | bytes 301064 | tf_op jit(solution)/shard_map/ppermute | solution.py:421
  28.0 7.6 %collective-permute-start.8 = (bf16[392,128]{1,0:T(8,128)(2,1)S(1)}, bf16[392,128]{1,0:T(8,128)(2,1)S(1)}, u32[]{:S(2)}, u32[]{:S(2)}) collective-permute-start(bf16[392,128]{1,0:T(8,128)(2,1)S(1)} %collective-permute-done.3.rest_4_), channel_id=1, source_target_pairs={{0,4},{4,0},{8,12},{12,8},{16,20},{20,16},{24,28},{28,24},{1,5},{5... | collective-permute-start | bytes 301064 | tf_op jit(solution)/shard_map/ppermute | solution.py:421
  29.5 7.1 %collective-permute-start.9 = (bf16[392,128]{1,0:T(8,128)(2,1)S(1)}, bf16[392,128]{1,0:T(8,128)(2,1)S(1)}, u32[]{:S(2)}, u32[]{:S(2)}) collective-permute-start(bf16[392,128]{1,0:T(8,128)(2,1)S(1)} %collective-permute-done.3.rest_4_), channel_id=1, source_target_pairs={{0,8},{4,12},{8,0},{12,4},{16,24},{20,28},{24,16},{28,20},{1,9},{5... | collective-permute-start | bytes 301064 | tf_op jit(solution)/shard_map/ppermute | solution.py:421
  33.9 2.8 %copy-start = (bf16[256,512]{1,0:T(8,128)(2,1)S(1)}, bf16[256,512]{1,0:T(8,128)(2,1)}, u32[]{:S(2)}) copy-start(bf16[256,512]{1,0:T(8,128)(2,1)} %constant.2.clone.table_ref) | copy-start | bytes 786436
  37.9 5.1 %collective-permute-start.14 = (bf16[64,512]{1,0:T(8,128)(2,1)S(1)}, bf16[64,512]{1,0:T(8,128)(2,1)S(1)}, u32[]{:S(2)}, u32[]{:S(2)}) collective-permute-start(bf16[64,512]{1,0:T(8,128)(2,1)S(1)} %get-tuple-element.40), channel_id=1, source_target_pairs={{0,1},{1,0},{2,3},{3,2},{4,5},{5,4},{6,7},{7,6},{8,9},{9,8},{10,11... | collective-permute-start | bytes 196616 | tf_op jit(solution)/shard_map/ppermute | solution.py:421
  38.0 5.0 %collective-permute-start.15 = (bf16[64,512]{1,0:T(8,128)(2,1)S(1)}, bf16[64,512]{1,0:T(8,128)(2,1)S(1)}, u32[]{:S(2)}, u32[]{:S(2)}) collective-permute-start(bf16[64,512]{1,0:T(8,128)(2,1)S(1)} %get-tuple-element.41), channel_id=1, source_target_pairs={{0,2},{1,3},{2,0},{3,1},{4,6},{5,7},{6,4},{7,5},{8,10},{9,11},{10,... | collective-permute-start | bytes 196616 | tf_op jit(solution)/shard_map/ppermute | solution.py:421
  39.5 4.1 %collective-permute-start.16 = (bf16[64,512]{1,0:T(8,128)(2,1)S(1)}, bf16[64,512]{1,0:T(8,128)(2,1)S(1)}, u32[]{:S(2)}, u32[]{:S(2)}) collective-permute-start(bf16[64,512]{1,0:T(8,128)(2,1)S(1)} %get-tuple-element.42), channel_id=1, source_target_pairs={{0,3},{1,2},{2,1},{3,0},{4,7},{5,6},{6,5},{7,4},{8,11},{9,10},{10,... | collective-permute-start | bytes 196616 | tf_op jit(solution)/shard_map/ppermute | solution.py:421
  41.1 2.5 %collective-permute-start.11 = (bf16[64,512]{1,0:T(8,128)(2,1)S(1)}, bf16[64,512]{1,0:T(8,128)(2,1)S(1)}, u32[]{:S(2)}, u32[]{:S(2)}) collective-permute-start(bf16[64,512]{1,0:T(8,128)(2,1)S(1)} %get-tuple-element.36), channel_id=1, source_target_pairs={{0,1},{1,0},{2,3},{3,2},{4,5},{5,4},{6,7},{7,6},{8,9},{9,8},{10,11... | collective-permute-start | bytes 196616 | tf_op jit(solution)/shard_map/ppermute | solution.py:421
  41.5 4.3 %collective-permute-start.12 = (bf16[64,512]{1,0:T(8,128)(2,1)S(1)}, bf16[64,512]{1,0:T(8,128)(2,1)S(1)}, u32[]{:S(2)}, u32[]{:S(2)}) collective-permute-start(bf16[64,512]{1,0:T(8,128)(2,1)S(1)} %get-tuple-element.37), channel_id=1, source_target_pairs={{0,2},{1,3},{2,0},{3,1},{4,6},{5,7},{6,4},{7,5},{8,10},{9,11},{10,... | collective-permute-start | bytes 196616 | tf_op jit(solution)/shard_map/ppermute | solution.py:421
  43.0 4.3 %collective-permute-start.13 = (bf16[64,512]{1,0:T(8,128)(2,1)S(1)}, bf16[64,512]{1,0:T(8,128)(2,1)S(1)}, u32[]{:S(2)}, u32[]{:S(2)}) collective-permute-start(bf16[64,512]{1,0:T(8,128)(2,1)S(1)} %get-tuple-element.38), channel_id=1, source_target_pairs={{0,3},{1,2},{2,1},{3,0},{4,7},{5,6},{6,5},{7,4},{8,11},{9,10},{10,... | collective-permute-start | bytes 196616 | tf_op jit(solution)/shard_map/ppermute | solution.py:421
